TPU v7x, 32 devices: a 4x4x1 block of a 4x4x8 slice. The times are simulated.
32 devices in a mesh: pairs: 1 (over z), ho: 4 (over y), tp: 8 (over x, core).
Axes of the slice: x: 4, y: 4, z: 1, core: 2. Of those that a mesh axis runs over, the one named last changes fastest.
The devices are a block of a 4x4x8 slice.
Arguments:
- prompts: bfloat16 [4, 2048, 4096], P('pairs')
- y_first: bfloat16 [4, 4096], P(('pairs', 'ho'))
- w_qkv: bfloat16 [2, 4096, 8, 6, 128], P(None, None, 'tp')
- w_o: bfloat16 [2, 4096, 4096], P(None, 'tp')
- w_gate: bfloat16 [2, 4096, 12288], P(None, None, 'tp')
- w_up: bfloat16 [2, 4096, 12288], P(None, None, 'tp')
- w_down: bfloat16 [2, 12288, 4096], P(None, 'tp')
- g_attn: float32 [2, 4096], replicated
- g_mlp: float32 [2, 4096], replicated
Outputs:
- output 1: bfloat16 [4, 2048, 4096], P(('pairs', 'ho'))
- output 2: float32 [4, 4096], P(('pairs', 'ho'))
- output 3: bfloat16 [4, 2, 2048, 8, 128], P(('pairs', 'ho'), None, 'tp')
- output 4: bfloat16 [4, 2, 2048, 8, 128], P(('pairs', 'ho'), None, 'tp')
- output 5: bfloat16 [4, 2, 2, 8, 128], P(('pairs', 'ho'), None, None, 'tp')
All inputs are finite; a program needn't handle non-finite values.
Results may differ from a plain program's by a relative error of at most 0.02.
Values are sent between devices in bfloat16 or wider.
A program may use at most 768 MiB of HBM per device.

v0:
```python
import jax
import jax.numpy as jnp
from jax import lax
from jax.sharding import PartitionSpec as P

NORM_EPS = 1e-5


def rms_norm(hidden, gain_vec):
    widened = hidden.astype(jnp.float32)
    inv_rms = lax.rsqrt(jnp.mean(widened * widened, axis=-1, keepdims=True) + NORM_EPS)
    return (widened * inv_rms * gain_vec).astype(jnp.bfloat16)


def mlp_part(h_mlp, w_gate, w_up, w_down):
    gate_pre = jnp.dot(h_mlp, w_gate, preferred_element_type=jnp.float32)
    up_pre = jnp.dot(h_mlp, w_up, preferred_element_type=jnp.float32)
    act_mid = (jax.nn.silu(gate_pre) * up_pre).astype(jnp.bfloat16)
    return jnp.dot(act_mid, w_down, preferred_element_type=jnp.float32).astype(jnp.bfloat16)


def prefill_layer(x_res, w_qkv, w_o, w_gate, w_up, w_down, g_attn, g_mlp):
    n_tok = x_res.shape[0]
    kv_loc, n_slots, head_dim = w_qkv.shape[1:]
    n_group = n_slots - 2
    h_norm = rms_norm(x_res, g_attn)
    qkv_out = jnp.einsum('td,dkgh->tkgh', h_norm, w_qkv, preferred_element_type=jnp.float32).astype(jnp.bfloat16)
    queries = qkv_out[:, :, :n_group]
    key_rows = qkv_out[:, :, n_group]
    val_rows = qkv_out[:, :, n_group + 1]
    scores = jnp.einsum('tkgh,skh->kgts', queries, key_rows, preferred_element_type=jnp.float32) * (head_dim ** -0.5)
    positions = jnp.arange(n_tok)
    scores = jnp.where(positions[:, None] >= positions[None, :], scores, -jnp.inf)
    weights = jnp.exp(scores - jnp.max(scores, axis=-1, keepdims=True))
    denom_sum = jnp.sum(weights, axis=-1, keepdims=True)
    numer_sum = jnp.einsum('kgts,skh->kgth', weights.astype(jnp.bfloat16), val_rows, preferred_element_type=jnp.float32)
    attn_out = (numer_sum / denom_sum).astype(jnp.bfloat16)
    w_o_heads = w_o.reshape(kv_loc, n_group, head_dim, w_o.shape[-1])
    proj_out = jnp.einsum('kgth,kghd->td', attn_out, w_o_heads, preferred_element_type=jnp.float32)
    x_res = x_res + lax.psum(proj_out.astype(jnp.bfloat16), 'tp')
    h_mlp = rms_norm(x_res, g_mlp)
    x_res = x_res + lax.psum(mlp_part(h_mlp, w_gate, w_up, w_down), 'tp')
    return x_res, key_rows, val_rows


def decode_layer(y_res, k_old, v_old, w_qkv, w_o, w_gate, w_up, w_down, g_attn, g_mlp):
    kv_loc, n_slots, head_dim = w_qkv.shape[1:]
    n_group = n_slots - 2
    attn_scale = head_dim ** -0.5
    h_norm = rms_norm(y_res, g_attn)
    qkv_loc = jnp.einsum('d,dkgh->kgh', h_norm, w_qkv, preferred_element_type=jnp.float32).astype(jnp.bfloat16)
    qkv_all = lax.all_gather(qkv_loc, 'tp', axis=0, tiled=True)
    q_new = qkv_all[:, :n_group]
    k_new = qkv_all[:, n_group]
    v_new = qkv_all[:, n_group + 1].astype(jnp.float32)
    s_old = jnp.einsum('kgh,tkh->kgt', q_new, k_old, preferred_element_type=jnp.float32) * attn_scale
    s_new = jnp.einsum('kgh,kh->kg', q_new, k_new, preferred_element_type=jnp.float32) * attn_scale
    top_score = jnp.maximum(lax.pmax(jnp.max(s_old, axis=-1), 'tp'), s_new)
    p_old = jnp.exp(s_old - top_score[:, :, None])
    numer_loc = jnp.einsum('kgt,tkh->kgh', p_old.astype(jnp.bfloat16), v_old, preferred_element_type=jnp.float32)
    numer_sum, denom_sum = lax.psum((numer_loc, jnp.sum(p_old, axis=-1)), 'tp')
    p_new = jnp.exp(s_new - top_score)
    numer_sum = numer_sum + p_new[:, :, None] * v_new[:, None, :]
    denom_sum = denom_sum + p_new
    attn_all = (numer_sum / denom_sum[:, :, None]).astype(jnp.bfloat16)
    n_tp = attn_all.shape[0] // kv_loc
    attn_loc = lax.dynamic_index_in_dim(attn_all.reshape(n_tp, kv_loc, n_group, head_dim), lax.axis_index('tp'), axis=0, keepdims=False)
    w_o_heads = w_o.reshape(kv_loc, n_group, head_dim, w_o.shape[-1])
    proj_out = jnp.einsum('kgh,kghd->d', attn_loc, w_o_heads, preferred_element_type=jnp.float32)
    y_res = y_res + lax.psum(proj_out.astype(jnp.bfloat16), 'tp').astype(jnp.float32)
    h_mlp = rms_norm(y_res, g_mlp)
    y_res = y_res + lax.psum(mlp_part(h_mlp, w_gate, w_up, w_down), 'tp').astype(jnp.float32)
    new_kv = jnp.stack([qkv_loc[:, n_group], qkv_loc[:, n_group + 1]])
    return y_res, new_kv


def solution(mesh):
    n_ho = mesh.shape['ho']
    shift_perm = [(src_idx, (src_idx + 1) % n_ho) for src_idx in range(n_ho)]
    row_axes = ('pairs', 'ho')
    in_specs = (P('pairs', None, None), P(row_axes, None), P(None, None, 'tp', None, None), P(None, 'tp', None), P(None, None, 'tp'), P(None, None, 'tp'), P(None, 'tp', None), P(None, None), P(None, None))
    out_specs = (P(row_axes, None, None), P(row_axes, None), P(row_axes, None, 'tp', None, None), P(row_axes, None, 'tp', None, None), P(row_axes, None, None, 'tp', None))

    def device_program(prompts, y_first, w_qkv, w_o, w_gate, w_up, w_down, g_attn, g_mlp):
        n_layers = w_qkv.shape[0]
        x_res = lax.dynamic_index_in_dim(prompts, lax.axis_index('ho'), axis=0, keepdims=False)
        k_list = []
        v_list = []
        for layer_idx in range(n_layers):
            x_res, key_rows, val_rows = prefill_layer(x_res, w_qkv[layer_idx], w_o[layer_idx], w_gate[layer_idx], w_up[layer_idx], w_down[layer_idx], g_attn[layer_idx], g_mlp[layer_idx])
            k_list.append(key_rows)
            v_list.append(val_rows)
        kv_heads = jnp.stack([jnp.stack(k_list), jnp.stack(v_list)])
        kv_tokens = lax.all_to_all(kv_heads, 'tp', 2, 3, tiled=True)
        kv_cache = lax.ppermute(kv_tokens, 'ho', perm=shift_perm)
        y_res = y_first[0].astype(jnp.float32)
        new_list = []
        for layer_idx in range(n_layers):
            y_res, new_kv = decode_layer(y_res, kv_cache[0, layer_idx], kv_cache[1, layer_idx], w_qkv[layer_idx], w_o[layer_idx], w_gate[layer_idx], w_up[layer_idx], w_down[layer_idx], g_attn[layer_idx], g_mlp[layer_idx])
            new_list.append(new_kv)
        return x_res[None], y_res[None], kv_cache[0][None], kv_cache[1][None], jnp.stack(new_list)[None]

    return jax.shard_map(device_program, mesh=mesh, in_specs=in_specs, out_specs=out_specs, check_vma=False)
```

profile of v0, /device:TPU:97, one launch (start us, length us, event | category | flops | bytes accessed | tf_op | source)
XLA Modules:
  0.0 1272.6 jit_solution(3459408323589167230)
XLA Ops:
  25.6 16.8 %fusion.96 = bf16[2048,1,6,128]{3,0,2,1:T(8,128)(2,1)S(1)} fusion(bf16[2,4096,1,6,128]{4,1,3,2,0:T(8,128)(2,1)S(1)} %bitcast.307, f32[4096]{0:T(1024)S(1)} %bitcast.329, f32[2048]{0:T(1024)S(1)} %add_rsqrt_fusion.3, bf16[4,2048,4096]{2,1,0:T(8,128)(2,1)} %param.9, s32[]{:T(128)S(6)} %select_n.16), kind=kOutput, calls=%fused_computation.99 | convolution fusion | flops 12920029184 | bytes 26238980 | tf_op jit(solution)/shard_map/td,dkgh->tkgh/dot_general | solution.py:27
  42.4 26.4 %fusion.4 = (f32[4,2048]{1,0:T(4,128)S(1)}, f32[2048,2048,4]{1,0,2:T(8,128)}) fusion(pred[2048,2048]{0,1:T(8,128)(4,1)} %iota_compare_fusion, bf16[2048,1,6,128]{3,0,2,1:T(8,128)(2,1)S(1)} %fusion.96), kind=kOutput, calls=%fused_computation.8 | convolution fusion | flops 4345290752 | bytes 73957376 | tf_op jit(solution)/shard_map/tkgh,skh->kgts/dot_general | solution.py:31
  68.8 22.9 %fusion = f32[4,2048]{1,0:T(4,128)S(1)} fusion(f32[2048,2048,4]{1,0,2:T(8,128)} %get-tuple-element.62, f32[4,2048]{1,0:T(4,128)S(1)} %get-tuple-element.61, pred[2048,2048]{0,1:T(8,128)(4,1)} %iota_compare_fusion), kind=kLoop, calls=%fused_computation.4 | loop fusion | flops 67100672 | bytes 71368704 | tf_op jit(solution)/shard_map/reduce_sum | solution.py:35
  91.8 27.4 %divide_convert_fusion.7 = bf16[4,2048,128]{2,1,0:T(8,128)(2,1)} fusion(f32[4,2048]{1,0:T(4,128)S(1)} %fusion, bf16[2048,1,6,128]{3,0,2,1:T(8,128)(2,1)S(1)} %fusion.96, f32[2048,2048,4]{1,0,2:T(8,128)} %get-tuple-element.62, f32[4,2048]{1,0:T(4,128)S(1)} %get-tuple-element.61, pred[2048,2048]{0,1:T(8,128)(4,1)} %iota_compare_fusion), kind=kOutput, calls=%fused_computation.96.clone.clone | convolution fusion | flops 4364173312 | bytes 73990144 | tf_op jit(solution)/shard_map/kgts,skh->kgth/dot_general | solution.py:36
  119.2 14.2 %bitcast_convert_fusion.1 = bf16[2048,4096]{1,0:T(8,128)(2,1)} fusion(bf16[4,128,4096]{2,1,0:T(8,128)(2,1)} %bitcast.304, bf16[4,2048,128]{2,1,0:T(8,128)(2,1)} %divide_convert_fusion.7), kind=kOutput, calls=%fused_computation.28 | convolution fusion | flops 8598323200 | bytes 23068672 | tf_op jit(solution)/shard_map/kgth,kghd->td/dot_general | solution.py:39
  134.8 180.0 %all-reduce.7.cloned.1.call-done = bf16[2048,4096]{1,0:T(8,128)(2,1)} async-done(((bf16[2048,4096]{1,0:T(8,128)(2,1)}), bf16[2048,4096]{1,0:T(8,128)(2,1)}) %all-reduce.7.cloned.1.call-update) | async-done | bytes 16777232 | tf_op jit(solution)/shard_map/psum | solution.py:40
  314.7 20.1 %fusion.6 = (f32[2048]{0:T(1024)S(1)}, bf16[2048,4096]{1,0:T(8,128)(2,1)}) fusion(bf16[2048,4096]{1,0:T(8,128)(2,1)} %all-reduce.7.cloned.1.call-done, bf16[4,2048,4096]{2,1,0:T(8,128)(2,1)} %param.9, s32[]{:T(128)S(6)} %select_n.16), kind=kLoop, calls=%fused_computation.16 | loop fusion | flops 33552384 | bytes 50339844 | tf_op jit(solution)/shard_map/reduce_sum | solution.py:11
  334.8 34.6 %fusion.50 = f32[2048,1536]{1,0:T(8,128)} fusion(bf16[2,4096,1536]{2,1,0:T(8,128)(2,1)} %param.14, bf16[2048,4096]{1,0:T(8,128)(2,1)} %get-tuple-element.40, f32[4096]{0:T(1024)S(1)} %bitcast.319, f32[2048]{0:T(1024)S(1)} %add_rsqrt_fusion.2), kind=kOutput, calls=%fused_computation.65 | convolution fusion | flops 25803358208 | bytes 41967616 | tf_op jit(solution)/shard_map/dot_general | solution.py:17
  369.4 36.4 %multiply_convert_fusion.2 = bf16[2048,1536]{1,0:T(8,128)(2,1)} fusion(f32[2048,1536]{1,0:T(8,128)} %fusion.50, bf16[2,4096,1536]{2,1,0:T(8,128)(2,1)} %param.13, bf16[2048,4096]{1,0:T(8,128)(2,1)} %get-tuple-element.40, f32[4096]{0:T(1024)S(1)} %bitcast.320, f32[2048]{0:T(1024)S(1)} %add_rsqrt_fusion.2), kind=kOutput, calls=%fused_computation.72 | convolution fusion | flops 25822232576 | bytes 48259072 | tf_op jit(solution)/shard_map/dot_general | solution.py:16
  405.8 32.8 %convolution_convert_fusion.1 = bf16[2048,4096]{1,0:T(8,128)(2,1)} fusion(bf16[2048,1536]{1,0:T(8,128)(2,1)} %multiply_convert_fusion.2, bf16[2,1536,4096]{2,1,0:T(8,128)(2,1)} %param.15), kind=kOutput, calls=%fused_computation.47 | convolution fusion | flops 25778192384 | bytes 35651584 | tf_op jit(solution)/shard_map/dot_general | solution.py:19
  438.8 177.8 %all-reduce.9.cloned.1.call-done = bf16[2048,4096]{1,0:T(8,128)(2,1)} async-done(((bf16[2048,4096]{1,0:T(8,128)(2,1)}), bf16[2048,4096]{1,0:T(8,128)(2,1)}) %all-reduce.9.cloned.1.call-update) | async-done | bytes 16777232 | tf_op jit(solution)/shard_map/psum | solution.py:42
  616.6 15.0 %fusion.9 = (f32[2048]{0:T(1024)S(1)}, bf16[2048,4096]{1,0:T(8,128)(2,1)S(1)}) fusion(bf16[2048,4096]{1,0:T(8,128)(2,1)} %get-tuple-element.40, bf16[2048,4096]{1,0:T(8,128)(2,1)} %all-reduce.9.cloned.1.call-done), kind=kLoop, calls=%fused_computation.19 | loop fusion | flops 33552384 | bytes 50339840 | tf_op jit(solution)/shard_map/reduce_sum | solution.py:11
  637.8 16.4 %fusion.101 = bf16[2048,1,6,128]{3,0,2,1:T(8,128)(2,1)S(1)} fusion(bf16[2,4096,1,6,128]{4,1,3,2,0:T(8,128)(2,1)} %param.11, bf16[2048,4096]{1,0:T(8,128)(2,1)S(1)} %get-tuple-element.38, f32[4096]{0:T(1024)S(1)} %bitcast.322, f32[2048]{0:T(1024)S(1)} %add_rsqrt_fusion.1), kind=kOutput, calls=%fused_computation.100 | convolution fusion | flops 12920029184 | bytes 26238976 | tf_op jit(solution)/shard_map/td,dkgh->tkgh/dot_general | solution.py:27
  654.2 25.6 %fusion.5 = (f32[4,2048]{1,0:T(4,128)S(1)}, f32[2048,2048,4]{1,0,2:T(8,128)}) fusion(pred[2048,2048]{0,1:T(8,128)(4,1)} %iota_compare_fusion, bf16[2048,1,6,128]{3,0,2,1:T(8,128)(2,1)S(1)} %fusion.101), kind=kOutput, calls=%fused_computation.9 | convolution fusion | flops 4345290752 | bytes 73957376 | tf_op jit(solution)/shard_map/tkgh,skh->kgts/dot_general | solution.py:31
  679.8 22.9 %fusion.2 = f32[4,2048]{1,0:T(4,128)S(1)} fusion(f32[2048,2048,4]{1,0,2:T(8,128)} %get-tuple-element.66, f32[4,2048]{1,0:T(4,128)S(1)} %get-tuple-element.65, pred[2048,2048]{0,1:T(8,128)(4,1)} %iota_compare_fusion), kind=kLoop, calls=%fused_computation.6 | loop fusion | flops 67100672 | bytes 71368704 | tf_op jit(solution)/shard_map/reduce_sum | solution.py:35
  702.7 27.4 %divide_convert_fusion.6 = bf16[4,2048,128]{2,1,0:T(8,128)(2,1)} fusion(f32[4,2048]{1,0:T(4,128)S(1)} %fusion.2, bf16[2048,1,6,128]{3,0,2,1:T(8,128)(2,1)S(1)} %fusion.101, f32[2048,2048,4]{1,0,2:T(8,128)} %get-tuple-element.66, f32[4,2048]{1,0:T(4,128)S(1)} %get-tuple-element.65, pred[2048,2048]{0,1:T(8,128)(4,1)} %iota_compare_fusion), kind=kOutput, calls=%fused_computation.95.clone.clone.1 | convolution fusion | flops 4364173312 | bytes 73990144 | tf_op jit(solution)/shard_map/kgts,skh->kgth/dot_general | solution.py:36
  758.9 41.8 %all_to_all.18 = bf16[2,2,2048,1,128]{4,1,3,0,2:T(2,128)(2,1)S(1)} all-to-all(bf16[2,2,2048,1,128]{4,1,3,0,2:T(2,128)(2,1)S(1)} %copy.28), channel_id=1, replica_groups=mesh['pairs'=1,'ho'=4,'tp'=8] {'tp'}, dimensions={2} | all-to-all | bytes 4194304 | tf_op jit(solution)/shard_map/all_to_all | solution.py:94
  809.1 18.6 %all-gather.2 = bf16[8,6,128]{2,1,0:T(8,128)(2,1)S(1)} all-gather(bf16[1,6,128]{2,1,0:T(8,128)(2,1)S(1)} %copy.67), channel_id=2, replica_groups=mesh['pairs'=1,'ho'=4,'tp'=8] {'tp'}, dimensions={0}, use_global_device_ids=true | all-gather | bytes 13824 | tf_op jit(solution)/shard_map/all_gather | solution.py:52
  827.9 21.9 %collective-permute-done = bf16[2,2,256,8,128]{4,2,3,1,0:T(8,128)(2,1)S(1)} collective-permute-done((bf16[2,2,256,8,128]{4,2,3,1,0:T(8,128)(2,1)}, bf16[2,2,256,8,128]{4,2,3,1,0:T(8,128)(2,1)S(1)}, u32[]{:S(2)}, u32[]{:S(2)}) %collective-permute-start) | collective-permute-done | bytes 2097184 | tf_op jit(solution)/shard_map/ppermute | solution.py:95
  864.1 21.1 %all-reduce.1 = (f32[8,4]{1,0:T(8,128)S(1)}, f32[8,4,128]{2,1,0:T(4,128)S(1)}) all-reduce(f32[8,4]{1,0:T(8,128)S(1)} %fusion.132, f32[8,4,128]{2,1,0:T(4,128)S(1)} %fusion.123), channel_id=1, replica_groups=mesh['pairs'=1,'ho'=4,'tp'=8] {'tp'}, use_global_device_ids=true, to_apply=%region_17.18 | all-reduce | flops 4128 | bytes 33024 | tf_op jit(solution)/shard_map/psum | solution.py:61
  888.1 15.9 %psum.90 = bf16[4096]{0:T(1024)(128)(2,1)S(1)} all-reduce(bf16[4096]{0:T(1024)(128)(2,1)S(1)} %convert_element_type.189), channel_id=1, replica_groups=mesh['pairs'=1,'ho'=4,'tp'=8] {'tp'}, use_global_device_ids=true, to_apply=%region_18.19 | all-reduce | flops 4096 | bytes 16384 | tf_op jit(solution)/shard_map/psum | solution.py:70
  912.3 33.1 %all-reduce.11.cloned.1.call-done = bf16[2048,4096]{1,0:T(8,128)(2,1)} async-done(((bf16[2048,4096]{1,0:T(8,128)(2,1)}), bf16[2048,4096]{1,0:T(8,128)(2,1)}) %all-reduce.11.cloned.1.call-update) | async-done | bytes 16777232 | tf_op jit(solution)/shard_map/psum | solution.py:40
  945.4 19.9 %fusion.12 = (f32[2048]{0:T(1024)S(1)}, bf16[2048,4096]{1,0:T(8,128)(2,1)}) fusion(bf16[2048,4096]{1,0:T(8,128)(2,1)} %copy-done, bf16[2048,4096]{1,0:T(8,128)(2,1)} %all-reduce.11.cloned.1.call-done), kind=kLoop, calls=%fused_computation.22 | loop fusion | flops 33552384 | bytes 50339840 | tf_op jit(solution)/shard_map/reduce_sum | solution.py:11
  965.3 34.6 %fusion.39 = f32[2048,1536]{1,0:T(8,128)} fusion(bf16[2,4096,1536]{2,1,0:T(8,128)(2,1)} %param.14, bf16[2048,4096]{1,0:T(8,128)(2,1)} %get-tuple-element.36, f32[4096]{0:T(1024)S(1)} %bitcast.316, f32[2048]{0:T(1024)S(1)} %add_rsqrt_fusion), kind=kOutput, calls=%fused_computation.54 | convolution fusion | flops 25803358208 | bytes 41967616 | tf_op jit(solution)/shard_map/dot_general | solution.py:17
  999.9 36.4 %multiply_convert_fusion.1 = bf16[2048,1536]{1,0:T(8,128)(2,1)} fusion(f32[2048,1536]{1,0:T(8,128)} %fusion.39, bf16[2,4096,1536]{2,1,0:T(8,128)(2,1)} %param.13, bf16[2048,4096]{1,0:T(8,128)(2,1)} %get-tuple-element.36, f32[4096]{0:T(1024)S(1)} %bitcast.317, f32[2048]{0:T(1024)S(1)} %add_rsqrt_fusion), kind=kOutput, calls=%fused_computation.71 | convolution fusion | flops 25822232576 | bytes 48259072 | tf_op jit(solution)/shard_map/dot_general | solution.py:16
  1036.3 33.0 %convolution_convert_fusion = bf16[2048,4096]{1,0:T(8,128)(2,1)} fusion(bf16[2048,1536]{1,0:T(8,128)(2,1)} %multiply_convert_fusion.1, bf16[2,1536,4096]{2,1,0:T(8,128)(2,1)} %param.15), kind=kOutput, calls=%fused_computation.46 | convolution fusion | flops 25778192384 | bytes 35651584 | tf_op jit(solution)/shard_map/dot_general | solution.py:19
  1099.9 19.1 %all-gather.3 = bf16[8,6,128]{2,1,0:T(8,128)(2,1)S(1)} all-gather(bf16[1,6,128]{2,1,0:T(8,128)(2,1)S(1)} %copy.68), channel_id=3, replica_groups=mesh['pairs'=1,'ho'=4,'tp'=8] {'tp'}, dimensions={0}, use_global_device_ids=true | all-gather | bytes 13824 | tf_op jit(solution)/shard_map/all_gather | solution.py:52
  1121.1 16.3 %pmax.15 = f32[8,4]{1,0:T(8,128)S(1)} all-reduce(f32[8,4]{1,0:T(8,128)S(1)} %get-tuple-element.67), channel_id=1, replica_groups=mesh['pairs'=1,'ho'=4,'tp'=8] {'tp'}, use_global_device_ids=true, to_apply=%region_23.24 | all-reduce | flops 32 | bytes 256 | tf_op jit(solution)/shard_map/pmax | solution.py:58
  1137.9 21.1 %all-reduce = (f32[8,4]{1,0:T(8,128)S(1)}, f32[8,4,128]{2,1,0:T(4,128)S(1)}) all-reduce(f32[8,4]{1,0:T(8,128)S(1)} %fusion.134, f32[8,4,128]{2,1,0:T(4,128)S(1)} %fusion.122), channel_id=1, replica_groups=mesh['pairs'=1,'ho'=4,'tp'=8] {'tp'}, use_global_device_ids=true, to_apply=%region_26.27 | all-reduce | flops 4128 | bytes 33024 | tf_op jit(solution)/shard_map/psum | solution.py:61
  1162.0 15.8 %psum.94 = bf16[4096]{0:T(1024)(128)(2,1)S(1)} all-reduce(bf16[4096]{0:T(1024)(128)(2,1)S(1)} %convert_element_type.200), channel_id=1, replica_groups=mesh['pairs'=1,'ho'=4,'tp'=8] {'tp'}, use_global_device_ids=true, to_apply=%region_27.28 | all-reduce | flops 4096 | bytes 16384 | tf_op jit(solution)/shard_map/psum | solution.py:70
  1212.0 36.7 %all-reduce.13.cloned.1.call-done = bf16[2048,4096]{1,0:T(8,128)(2,1)} async-done(((bf16[2048,4096]{1,0:T(8,128)(2,1)}), bf16[2048,4096]{1,0:T(8,128)(2,1)}) %all-reduce.13.cloned.1.call-update) | async-done | bytes 16777232 | tf_op jit(solution)/shard_map/psum | solution.py:42
  1248.7 17.2 %add_bitcast_fusion = bf16[1,2048,4096]{2,1,0:T(8,128)(2,1)} fusion(bf16[2048,4096]{1,0:T(8,128)(2,1)} %get-tuple-element.36, bf16[2048,4096]{1,0:T(8,128)(2,1)} %all-reduce.13.cloned.1.call-done), kind=kLoop, calls=%fused_computation.40 | loop fusion | flops 8388608 | bytes 50331648 | tf_op jit(solution)/shard_map/broadcast_in_dim | solution.py:101
  (145 shorter events, 156.1 us)
Async XLA Ops:
  7.2 13.0 %copy-start.11 = (f32[2,4096]{1,0:T(2,128)S(1)}, f32[2,4096]{1,0:T(2,128)}, u32[]{:S(2)}) copy-start(f32[2,4096]{1,0:T(2,128)} %param.16) | copy-start | bytes 98308
  7.2 307.5 %all-reduce.7.cloned.1.call-start = ((), (), s32[]{:S(2)}) async-start(), calls=%async_computation.1 | async-start | bytes 33554432 | tf_op jit(solution)/shard_map/psum | solution.py:40
  11.3 9.5 copy-start.1
  11.3 13.7 %slice-start = ((s8[12582912]{0:T(1024)(128)(4,1)}), s8[4194304]{0:T(1024)(128)(4,1)S(1)}, s32[]{:S(2)}) async-start(s8[12582912]{0:T(1024)(128)(4,1)} %bitcast.306), calls=%async_computation.5 | async-start | bytes 8388608
  11.3 13.7 %slice-start.1 = ((s8[12582912]{0:T(1024)(128)(4,1)}), s8[4194304]{0:T(1024)(128)(4,1)S(1)}, s32[]{:S(2)}) async-start(s8[12582912]{0:T(1024)(128)(4,1)} %bitcast.306), calls=%async_computation.6 | async-start | bytes 8388608
  20.8 4.7 slice-start.2
  42.4 49.4 %copy-start.6 = (bf16[2048,1,6,128]{3,0,2,1:T(8,128)(2,1)}, bf16[2048,1,6,128]{3,0,2,1:T(8,128)(2,1)S(1)}, u32[]{:S(2)}) copy-start(bf16[2048,1,6,128]{3,0,2,1:T(8,128)(2,1)S(1)} %fusion.96) | copy-start | bytes 9437188
  133.4 0.8 copy-start.19
  133.4 483.2 %all-reduce.9.cloned.1.call-start = ((), (), s32[]{:S(2)}) async-start(), calls=%async_computation.2 | async-start | bytes 33554432 | tf_op jit(solution)/shard_map/psum | solution.py:42
  134.8 234.7 %copy-start.14 = (f32[1,4096]{1,0:T(1,128)}, f32[1,4096]{1,0:T(1,128)S(1)}, u32[]{:S(2)}) copy-start(f32[1,4096]{1,0:T(1,128)S(1)} %get-tuple-element.50) | copy-start | bytes 49156
  438.7 199.1 %copy-start.16 = (f32[1,4096]{1,0:T(1,128)S(1)}, f32[1,4096]{1,0:T(1,128)}, u32[]{:S(2)}) copy-start(f32[1,4096]{1,0:T(1,128)} %get-tuple-element.51) | copy-start | bytes 49156
  438.7 506.7 %all-reduce.11.cloned.1.call-start = ((), (), s32[]{:S(2)}) async-start(), calls=%async_computation.3 | async-start | bytes 33554432 | tf_op jit(solution)/shard_map/psum | solution.py:40
  631.6 6.2 copy-start
  744.3 59.2 %copy-start.18 = (bf16[1,4096]{1,0:T(2,128)(2,1)S(1)}, bf16[1,4096]{1,0:T(2,128)(2,1)}, u32[]{:S(2)}) copy-start(bf16[1,4096]{1,0:T(2,128)(2,1)} %param.10) | copy-start | bytes 24580
  744.3 60.6 %copy-start.12 = (f32[2,4096]{1,0:T(2,128)S(1)}, f32[2,4096]{1,0:T(2,128)}, u32[]{:S(2)}) copy-start(f32[2,4096]{1,0:T(2,128)} %param.16) | copy-start | bytes 98308
  744.3 504.4 %all-reduce.13.cloned.1.call-start = ((), (), s32[]{:S(2)}) async-start(), calls=%async_computation.4 | async-start | bytes 33554432 | tf_op jit(solution)/shard_map/psum | solution.py:42
  745.8 159.5 %copy-start.15 = (f32[1,4096]{1,0:T(1,128)S(1)}, f32[1,4096]{1,0:T(1,128)}, u32[]{:S(2)}) copy-start(f32[1,4096]{1,0:T(1,128)} %copy-done.14) | copy-start | bytes 49156
  802.3 47.5 %collective-permute-start = (bf16[2,2,256,8,128]{4,2,3,1,0:T(8,128)(2,1)}, bf16[2,2,256,8,128]{4,2,3,1,0:T(8,128)(2,1)S(1)}, u32[]{:S(2)}, u32[]{:S(2)}) collective-permute-start(bf16[2,2,256,8,128]{4,2,3,1,0:T(8,128)(2,1)} %bitcast.50), channel_id=1, source_target_pairs={{0,8},{8,16},{16,24},{24,0},{1,9},{9,17},{17,25},{25,1},{2,10},{10... | collective-permute-start | bytes 6291464 | tf_op jit(solution)/shard_map/ppermute | solution.py:95
  803.5 161.8 %copy-start.4 = (f32[1,4096]{1,0:T(1,128)}, f32[1,4096]{1,0:T(1,128)S(1)}, u32[]{:S(2)}) copy-start(f32[1,4096]{1,0:T(1,128)S(1)} %convert_element_type.206) | copy-start | bytes 49156
  849.8 115.5 %copy-start.2 = (bf16[2,2,256,8,128]{4,2,3,1,0:T(8,128)(2,1)}, bf16[2,2,256,8,128]{4,2,3,1,0:T(8,128)(2,1)S(1)}, u32[]{:S(2)}) copy-start(bf16[2,2,256,8,128]{4,2,3,1,0:T(8,128)(2,1)S(1)} %collective-permute-done) | copy-start | bytes 6291460
  904.0 61.3 %copy-start.9 = (bf16[4096]{0:T(1024)(128)(2,1)}, bf16[4096]{0:T(1024)(128)(2,1)S(1)}, u32[]{:S(2)}) copy-start(bf16[4096]{0:T(1024)(128)(2,1)S(1)} %psum.90) | copy-start | bytes 24580
  905.4 0.6 copy-start.7
  912.3 53.0 %copy-start.13 = (f32[1,4096]{1,0:T(1,128)S(1)}, f32[1,4096]{1,0:T(1,128)}, u32[]{:S(2)}) copy-start(f32[1,4096]{1,0:T(1,128)} %get-tuple-element.49) | copy-start | bytes 49156
  1069.3 0.7 copy-start.8
  1069.3 6.4 copy-start.20
  1070.0 24.8 %copy-start.5 = (f32[1,4096]{1,0:T(1,128)S(1)}, f32[1,4096]{1,0:T(1,128)}, u32[]{:S(2)}) copy-start(f32[1,4096]{1,0:T(1,128)} %copy-done.4) | copy-start | bytes 49156
  1070.0 24.8 %copy-start.10 = (bf16[4096]{0:T(1024)(128)(2,1)S(1)}, bf16[4096]{0:T(1024)(128)(2,1)}, u32[]{:S(2)}) copy-start(bf16[4096]{0:T(1024)(128)(2,1)} %copy-done.9) | copy-start | bytes 24580
  1070.0 26.1 %copy-start.17 = (f32[1,4096]{1,0:T(1,128)S(1)}, f32[1,4096]{1,0:T(1,128)}, u32[]{:S(2)}) copy-start(f32[1,4096]{1,0:T(1,128)} %get-tuple-element.51) | copy-start | bytes 49156
  1070.0 49.0 %copy-start.3 = (bf16[2,2,256,8,128]{4,2,3,1,0:T(8,128)(2,1)S(1)}, bf16[2,2,256,8,128]{4,2,3,1,0:T(8,128)(2,1)}, u32[]{:S(2)}) copy-start(bf16[2,2,256,8,128]{4,2,3,1,0:T(8,128)(2,1)} %copy-done.2) | copy-start | bytes 6291460
  1185.0 25.9 %copy-start.21 = (bf16[2,1,128]{2,0,1:T(2,128)(2,1)S(1)}, bf16[2,1,128]{2,0,1:T(2,128)(2,1)}, u32[]{:S(2)}) copy-start(bf16[2,1,128]{2,0,1:T(2,128)(2,1)} %copy.72) | copy-start | bytes 1540
Sparse Core Ops, SparseCore 0:
  133.6 181.1 all-reduce.6
  438.8 177.7 all-reduce.8
  744.4 200.9 all-reduce.10
  1069.5 179.1 all-reduce.12
where the time goes:
time: 1280 us; the launch traced here: 1270 us
  waiting for transfers between devices  450 us (35%)
  matrix products  425 us (33%)
  blocking collectives  210 us (16%)
  other arithmetic  136 us (11%)
  local copies, waits for them, and re-layouts  34 us (3%)
  between operations  17.3 us (1%)
    psum x2, waiting for transfers between devices, prefill_layer(): x_res = x_res + lax.psum(mlp_part(h_mlp, w_gate, w_up, w_down), 'tp')  215 us
    psum x2, waiting for transfers between devices, prefill_layer(): x_res = x_res + lax.psum(proj_out.astype(jnp.bfloat16), 'tp')  213 us
    dot_general x4, matrix products, mlp_part(): gate_pre = jnp.dot(h_mlp, w_gate, preferred_element_type=jnp.float32)  84 us
    dot_general x4, matrix products, mlp_part(): up_pre = jnp.dot(h_mlp, w_up, preferred_element_type=jnp.float32)  81.3 us
    dot_general x4, matrix products, mlp_part(): jnp.dot(act_mid, w_down, preferred_element_type=jnp.float32)  76.8 us
    reduce_sum x8, other arithmetic, rms_norm(): jnp.mean(widened * widened, axis=-1, keepdims=True) + NORM_EPS  66.3 us
    dot_general x2, matrix products, prefill_layer(): jnp.einsum('kgts,skh->kgth', weights.astype(jnp.bfloat16), val_rows, pref...  54.9 us
    dot_general x2, matrix products, prefill_layer(): jnp.einsum('tkgh,skh->kgts', queries, key_rows, preferred_element_type=jn...  52 us
  transfers between devices with their start and end apart: 5, of which 5 were waited for; matrix products, arithmetic and copies ran while one was open for 6% of the time, Pallas kernels for 0%

commit v1 on v0

v1 whole, which is shorter than its diff:
```python
import functools

import jax
import jax.numpy as jnp
from jax import lax
from jax.experimental import pallas as pl
from jax.experimental.pallas import tpu as pltpu
from jax.sharding import PartitionSpec as P

NORM_EPS = 1e-5
MESH = pl.DeviceIdType.MESH
CHUNKS = 8
PAD = 16
COLS_A = 256
COLS_B = 512
LAGS = 6
F32 = jnp.float32
BF16 = jnp.bfloat16


def norm_rows(rows_f32, gain):
    inv_rms = lax.rsqrt(jnp.mean(rows_f32 * rows_f32, axis=-1, keepdims=True) + NORM_EPS)
    return (rows_f32 * inv_rms * gain).astype(BF16)


def remote(src, dst, send, recv, device):
    return pltpu.make_async_remote_copy(src_ref=src, dst_ref=dst, send_sem=send, recv_sem=recv, device_id=device, device_id_type=MESH)


def group_kernel(n_ho, n_tp, prompts, y_first, w_qkv, w_o, w_gate, w_up, w_down, gains, x_last, tail, kv_tok,
                 hid, part, pair_in, ring1, ring2, resid, kv, scores, qry, att, act, stage, wa, wb, cb0, cb1,
                 k_new, v_new, y_row, y_part, y_pair, y_chip, tail_out, tail_in,
                 wa_sem, wb_sem, in_sem, out_sem, pair_s, pair_r, r1_s, r1_r, r2_s, r2_r, a1_s, a1_r, a2_s, a2_r, d_s, d_r,
                 yp_s, yp_r, yc_s, yc_r, edge_s, edge_r, c0_s, c0_r, c1_s, c1_r, c2_s, c2_r, c2_l):
    tp = lax.axis_index("tp")
    ho = lax.axis_index("ho")
    n_chip = n_tp // 2
    core = lax.rem(tp, 2)
    chip = lax.div(tp, 2)
    to_right = {"tp": lax.rem(tp + 2, n_tp)}
    to_left = {"tp": lax.rem(tp + n_tp - 2, n_tp)}
    to_far = {"tp": lax.rem(tp + 4, n_tp)}
    to_pair = {"tp": tp + 1 - 2 * core}
    to_up = {"ho": lax.rem(ho + 1, n_ho)}
    to_down = {"ho": lax.rem(ho + n_ho - 1, n_ho)}
    c_right = lax.rem(chip + 1, n_chip)
    c_left = lax.rem(chip + n_chip - 1, n_chip)
    c_far = lax.rem(chip + 2, n_chip)

    n_layers, n_slots, d_model, head = w_qkv.shape
    n_group = n_slots - 2
    ff = w_gate.shape[2]
    n_tok = prompts.shape[1]
    rows = n_tok // CHUNKS
    half = rows // 2
    own = half // n_chip
    sub = own // 2
    all_rows = rows + PAD
    n_stage = 2 * n_layers
    n_steps = n_stage * CHUNKS
    t_qkv = n_slots * head // COLS_A
    t_gu = ff // COLS_A
    t_out = d_model // COLS_B
    mine = pl.multiple_of(core * half, half)
    theirs = pl.multiple_of(half - core * half, half)
    tok_dev = n_tok // n_tp
    tok_chip = 2 * tok_dev
    scale = head ** -0.5

    def block(base, which):
        return pl.multiple_of(base + which * own, own)

    barrier = pltpu.get_barrier_semaphore()
    peers = (to_right, to_left, to_far, to_pair, to_up, to_down)
    for peer in peers:
        pl.semaphore_signal(barrier, inc=1, device_id=peer, device_id_type=MESH)
    pl.semaphore_wait(barrier, len(peers))

    def qkv_copy(layer, t, u):
        return pltpu.make_async_copy(w_qkv.at[layer, t * 2 + u], wa.at[t, :, pl.ds(u * head, head)], wa_sem.at[t, u])

    def gu_copy(layer, t, u):
        slot = lax.rem(t, 2) * 2 + u
        cols = pl.ds(pl.multiple_of(t * COLS_A, COLS_A), COLS_A)
        return pltpu.make_async_copy((w_gate, w_up)[u].at[layer, :, cols], wa.at[slot], wa_sem.at[slot, 0])

    def out_copy(layer, t):
        slot = lax.rem(t, 3)
        cols = pl.ds(pl.multiple_of(t * COLS_B, COLS_B), COLS_B)
        return pltpu.make_async_copy(w_o.at[layer, :, cols], wb.at[slot, pl.ds(0, n_group * head)], wb_sem.at[slot])

    def down_copy(layer, t):
        slot = lax.rem(t, 3)
        cols = pl.ds(pl.multiple_of(t * COLS_B, COLS_B), COLS_B)
        return pltpu.make_async_copy(w_down.at[layer, :, cols], wb.at[slot], wb_sem.at[slot])

    def prompt_copy(c):
        return pltpu.make_async_copy(prompts.at[ho, pl.ds(pl.multiple_of(c * rows, rows), rows)], stage, in_sem)

    def prefetch(step):
        st = lax.div(step, CHUNKS)
        layer = lax.div(st, 2)

        @pl.when(st == 0)
        def _():
            prompt_copy(lax.rem(step, CHUNKS)).start()

        @pl.when(lax.rem(st, 2) == 0)
        def _():
            for t in range(t_qkv):
                for u in range(2):
                    qkv_copy(layer, t, u).start()
            for t in range(3):
                out_copy(layer, t).start()

        @pl.when(lax.rem(st, 2) == 1)
        def _():
            for t in range(2):
                for u in range(2):
                    gu_copy(layer, t, u).start()
            for t in range(3):
                down_copy(layer, t).start()

    def pair_copy(g):
        s = lax.rem(g, 2)
        return remote(part.at[lax.rem(g, 3), pl.ds(theirs, half)], pair_in.at[s], pair_s.at[s], pair_r.at[s], to_pair)

    def r1_copy(g, d):
        s = lax.rem(g, 2)
        base = pl.multiple_of(block(mine, c_far) + d * sub, sub)
        return remote(part.at[lax.rem(g, 3), pl.ds(base, sub)], ring1.at[s, d], r1_s.at[d], r1_r.at[s, d], (to_right, to_left)[d])

    def r2_copy(g, d):
        s = lax.rem(g, 2)
        base = block(mine, (c_right, c_left)[d])
        return remote(part.at[lax.rem(g, 3), pl.ds(base, own)], ring2.at[s, d], r2_s.at[d], r2_r.at[s, d], (to_right, to_left)[d])

    def a1_copy(g, d):
        c = lax.rem(g, CHUNKS)
        ref = hid.at[c, pl.ds(block(mine, chip), own)]
        return remote(ref, ref, a1_s.at[d], a1_r.at[c, d], (to_right, to_left)[d])

    def a2_copy(g, d):
        c = lax.rem(g, CHUNKS)
        base = pl.multiple_of(block(mine, (c_left, c_right)[d]) + d * sub, sub)
        ref = hid.at[c, pl.ds(base, sub)]
        return remote(ref, ref, a2_s.at[d], a2_r.at[c, d], (to_right, to_left)[d])

    def d_copy(g, i):
        c = lax.rem(g, CHUNKS)
        ref = hid.at[c, pl.ds(block(mine, (chip, c_left, c_right, c_far)[i]), own)]
        return remote(ref, ref, d_s.at[i], d_r.at[c, i], to_pair)

    def last_copy(c):
        return pltpu.make_async_copy(hid.at[c, pl.ds(0, rows)], x_last.at[pl.ds(pl.multiple_of(c * rows, rows), rows)], out_sem.at[c])

    def when_chunk(g, body):
        @pl.when(jnp.logical_and(g >= 0, g < n_steps))
        def _():
            body(g)

    def e1(g):
        pair_copy(g).wait_recv()
        pair_copy(g).wait_send()
        slot = lax.rem(g, 3)
        s = lax.rem(g, 2)

        @pl.loop(0, half // PAD)
        def _(i):
            dst = pl.ds(pl.multiple_of(mine + i * PAD, PAD), PAD)
            src = pl.ds(pl.multiple_of(i * PAD, PAD), PAD)
            part[slot, dst] = (part[slot, dst].astype(F32) + pair_in[s, src].astype(F32)).astype(BF16)

        for d in range(2):
            r1_copy(g, d).start()

    def e2(g):
        slot = lax.rem(g, 3)
        s = lax.rem(g, 2)
        for d in range(2):
            r1_copy(g, d).wait_send()
            r1_copy(g, d).wait_recv()
            dst = pl.ds(pl.multiple_of(block(mine, (c_right, c_left)[d]) + d * sub, sub), sub)
            part[slot, dst] = (part[slot, dst].astype(F32) + ring1[s, d].astype(F32)).astype(BF16)
            r2_copy(g, d).start()

    def e3(g):
        slot = lax.rem(g, 3)
        s = lax.rem(g, 2)
        c = lax.rem(g, CHUNKS)
        st = lax.div(g, CHUNKS)
        for d in range(2):
            r2_copy(g, d).wait_send()
            r2_copy(g, d).wait_recv()
        base = block(mine, chip)

        def new_rows(i):
            loc = pl.ds(i * PAD, PAD)
            dst = pl.ds(pl.multiple_of(base + i * PAD, PAD), PAD)
            total = part[slot, dst].astype(F32) + ring2[s, 0, loc].astype(F32) + ring2[s, 1, loc].astype(F32)
            return loc, dst, (resid[c, loc].astype(F32) + total.astype(BF16).astype(F32)).astype(BF16)

        @pl.when(st < n_stage - 1)
        def _():
            gain = gains[jnp.minimum(st + 1, n_stage - 1)]
            for i in range(own // PAD):
                loc, dst, new = new_rows(i)
                resid[c, loc] = new
                hid[c, dst] = norm_rows(new.astype(F32), gain)

        @pl.when(st == n_stage - 1)
        def _():
            for i in range(own // PAD):
                _, dst, new = new_rows(i)
                hid[c, dst] = new

        for d in range(2):
            a1_copy(g, d).start()
        d_copy(g, 0).start()

    def e4(g):
        for d in range(2):
            a1_copy(g, d).wait_send()
            a1_copy(g, d).wait_recv()
            a2_copy(g, d).start()
        d_copy(g, 0).wait_send()
        d_copy(g, 1).start()
        d_copy(g, 2).start()

    def e5(g):
        for d in range(2):
            a2_copy(g, d).wait_send()
            a2_copy(g, d).wait_recv()
        d_copy(g, 1).wait_send()
        d_copy(g, 2).wait_send()
        d_copy(g, 3).start()

    def e6(g):
        d_copy(g, 3).wait_send()
        for i in range(4):
            d_copy(g, i).wait_recv()

        @pl.when(g >= n_steps - CHUNKS)
        def _():
            last_copy(lax.rem(g, CHUNKS)).start()

    def y_pair_copy(st):
        return remote(y_part.at[st], y_pair.at[st], yp_s.at[st], yp_r.at[st], to_pair)

    def y_chip_copy(st, i):
        src_chip = chip
        return remote(y_chip.at[st, src_chip], y_chip.at[st, src_chip], yc_s.at[i], yc_r.at[st, i], (to_right, to_left, to_far)[i])

    first_copy = remote(y_first, y_row, edge_s.at[0], edge_r.at[0], to_down)
    tail_copy = remote(tail_out, tail_in, edge_s.at[1], edge_r.at[1], to_up)

    def put_y(gain):
        row = norm_rows(y_row[...], gain)
        hid[CHUNKS - 1, pl.ds(rows, PAD)] = jnp.broadcast_to(row.astype(F32), (PAD, d_model)).astype(BF16)

    def y_sum(st):
        y_pair_copy(st).wait_send()
        y_pair_copy(st).wait_recv()
        y_chip[st, chip] = y_part[st] + y_pair[st]
        for i in range(3):
            y_chip_copy(st, i).start()

    def y_done(st):
        for i in range(3):
            y_chip_copy(st, i).wait_send()
            y_chip_copy(st, i).wait_recv()
        total = y_chip[st, 0]
        for i in range(1, n_chip):
            total = total + y_chip[st, i]
        y_row[...] = y_row[...] + total.astype(BF16).astype(F32)

        @pl.when(st < n_stage - 1)
        def _():
            put_y(gains[jnp.minimum(st + 1, n_stage - 1)])

        @pl.when(st == n_stage - 1)
        def _():
            tail_out[:, pl.ds(0, d_model)] = y_row[...]
            tail_copy.start()

    def c0_copy(layer):
        return remote(kv.at[layer], cb0.at[layer], c0_s.at[layer], c0_r.at[layer], to_up)

    def c1_copy(layer, i):
        dst_chip = (c_right, c_left, c_far)[i]
        src = cb0.at[layer, :, pl.ds(pl.multiple_of(dst_chip * tok_chip, tok_chip), tok_chip)]
        return remote(src, cb1.at[layer, i], c1_s.at[layer, i], c1_r.at[layer, i], (to_right, to_left, to_far)[i])

    def c2_source(layer, i, which):
        off = pl.multiple_of(which * tok_dev, tok_dev)
        if i < 3:
            return cb1.at[layer, i, :, pl.ds(off, tok_dev)], (c_left, c_right, c_far)[i]
        return cb0.at[layer, :, pl.ds(pl.multiple_of(chip * tok_chip + off, tok_dev), tok_dev)], chip

    def c2_copy(layer, i):
        src, src_chip = c2_source(layer, i, 1 - core)
        return remote(src, kv_tok.at[layer, :, 2 * src_chip + core], c2_s.at[layer, i], c2_r.at[layer, i], to_pair)

    def c2_local(layer, i):
        src, src_chip = c2_source(layer, i, core)
        return pltpu.make_async_copy(src, kv_tok.at[layer, :, 2 * src_chip + core], c2_l.at[layer, i])

    def cache_events(g):
        for layer in range(n_layers):
            at = (2 * layer + 1) * CHUNKS

            @pl.when(g == at)
            def _():
                c0_copy(layer).start()

            @pl.when(g == at + 2)
            def _():
                c0_copy(layer).wait_send()
                c0_copy(layer).wait_recv()
                c1_copy(layer, 0).start()
                c1_copy(layer, 1).start()

            @pl.when(g == at + 3)
            def _():
                c1_copy(layer, 2).start()

            @pl.when(g == at + 5)
            def _():
                for i in range(3):
                    c1_copy(layer, i).wait_send()
                    c1_copy(layer, i).wait_recv()
                for i in range(4):
                    c2_copy(layer, i).start()
                    c2_local(layer, i).start()

            @pl.when(g == at + 7)
            def _():
                for i in range(4):
                    c2_copy(layer, i).wait_send()
                    c2_copy(layer, i).wait_recv()
                    c2_local(layer, i).wait()

    def store_part(g, t, acc):
        cols = pl.ds(pl.multiple_of(t * COLS_B, COLS_B), COLS_B)
        part[lax.rem(g, 3), :, cols] = acc[:rows].astype(BF16)
        y_part[lax.div(g, CHUNKS), :, cols] = acc[rows:rows + 1]

    def first_norm(c):
        prompt_copy(c).wait()
        gain = gains[0]

        @pl.loop(0, rows // PAD)
        def _(i):
            loc = pl.ds(pl.multiple_of(i * PAD, PAD), PAD)
            hid[c, loc] = norm_rows(stage[loc].astype(F32), gain)

        for i in range(own // PAD):
            resid[c, pl.ds(i * PAD, PAD)] = stage[pl.ds(pl.multiple_of(block(mine, chip) + i * PAD, PAD), PAD)]

        @pl.when(c == CHUNKS - 1)
        def _():
            first_copy.wait_send()
            first_copy.wait_recv()
            put_y(gain)

    def attention(layer, c):
        below = lax.broadcasted_iota(jnp.int32, (rows, rows), 0) - lax.broadcasted_iota(jnp.int32, (rows, rows), 1)
        for h in range(n_group):
            q = qry[pl.ds(0, rows), pl.ds(h * head, head)]

            def scores_of(j, top):
                loc = pl.ds(pl.multiple_of(j * rows, rows), rows)
                s = lax.dot_general(q, kv[layer, 0, loc], (((1,), (1,)), ((), ())), preferred_element_type=F32) * scale
                s = jnp.where(below >= (j - c) * rows, s, -jnp.inf)
                scores[:, loc] = s
                for b in range(rows // head):
                    top = jnp.maximum(top, s[:, b * head:(b + 1) * head])
                return top

            top = lax.fori_loop(0, c + 1, scores_of, jnp.full((rows, head), -jnp.inf, F32))
            top = jnp.max(top, axis=1, keepdims=True)

            def sums_of(j, carry):
                denom, numer = carry
                loc = pl.ds(pl.multiple_of(j * rows, rows), rows)
                p = jnp.exp(scores[:, loc] - top)
                for b in range(rows // head):
                    denom = denom + p[:, b * head:(b + 1) * head]
                return denom, numer + jnp.dot(p.astype(BF16), kv[layer, 1, loc], preferred_element_type=F32)

            zero = jnp.zeros((rows, head), F32)
            denom, numer = lax.fori_loop(0, c + 1, sums_of, (zero, zero))
            att[pl.ds(0, rows), pl.ds(h * head, head)] = (numer / jnp.sum(denom, axis=1, keepdims=True)).astype(BF16)

    def attention_new(layer):
        k_row = k_new[...].astype(F32)
        v_row = v_new[...].astype(F32)
        for h in range(n_group):
            q = qry[pl.ds(rows, PAD), pl.ds(h * head, head)]
            s_new = jnp.sum(q.astype(F32) * k_row, axis=1, keepdims=True) * scale

            def scores_of(j, top):
                loc = pl.ds(pl.multiple_of(j * rows, rows), rows)
                s = lax.dot_general(q, kv[layer, 0, loc], (((1,), (1,)), ((), ())), preferred_element_type=F32) * scale
                scores[pl.ds(0, PAD), loc] = s
                return jnp.maximum(top, jnp.max(s, axis=1, keepdims=True))

            top = lax.fori_loop(0, CHUNKS, scores_of, s_new)

            def sums_of(j, carry):
                denom, numer = carry
                loc = pl.ds(pl.multiple_of(j * rows, rows), rows)
                p = jnp.exp(scores[pl.ds(0, PAD), loc] - top)
                denom = denom + jnp.sum(p, axis=1, keepdims=True)
                return denom, numer + jnp.dot(p.astype(BF16), kv[layer, 1, loc], preferred_element_type=F32)

            p_new = jnp.exp(s_new - top)
            denom, numer = lax.fori_loop(0, CHUNKS, sums_of, (p_new, p_new * v_row))
            att[pl.ds(rows, PAD), pl.ds(h * head, head)] = (numer / denom).astype(BF16)

    def step_a(g, layer, c):
        @pl.when(layer == 0)
        def _():
            first_norm(c)

        for t in range(t_qkv):
            for u in range(2):
                qkv_copy(layer, t, u).wait()
            out = jnp.dot(hid[c], wa[t], preferred_element_type=F32).astype(BF16)
            if t < t_qkv - 1:
                qry[:, pl.ds(t * COLS_A, COLS_A)] = out
            else:
                loc = pl.ds(pl.multiple_of(c * rows, rows), rows)
                kv[layer, 0, loc] = out[:rows, :head]
                kv[layer, 1, loc] = out[:rows, head:]
                k_new[...] = out[rows:, :head]
                v_new[...] = out[rows:, head:]
        when_chunk(g - 1, e1)
        attention(layer, c)

        @pl.when(c == CHUNKS - 1)
        def _():
            attention_new(layer)
            for ll in range(n_layers):
                @pl.when(layer == ll)
                def _():
                    tail_out[:, pl.ds(d_model + 2 * ll * head, head)] = k_new[...].astype(F32)[:1]
                    tail_out[:, pl.ds(d_model + (2 * ll + 1) * head, head)] = v_new[...].astype(F32)[:1]

        @pl.loop(0, t_out)
        def _(t):
            out_copy(layer, t).wait()
            slot = lax.rem(t, 3)
            store_part(g, t, jnp.dot(att[...], wb[slot, :n_group * head], preferred_element_type=F32))

            @pl.when(t + 3 < t_out)
            def _():
                out_copy(layer, t + 3).start()

    def step_m(g, layer, c):
        @pl.loop(0, t_gu)
        def _(t):
            for u in range(2):
                gu_copy(layer, t, u).wait()
            slot = lax.rem(t, 2) * 2
            gate = jnp.dot(hid[c], wa[slot], preferred_element_type=F32)
            up = jnp.dot(hid[c], wa[slot + 1], preferred_element_type=F32)
            act[:, pl.ds(pl.multiple_of(t * COLS_A, COLS_A), COLS_A)] = (jax.nn.silu(gate) * up).astype(BF16)

            @pl.when(t + 2 < t_gu)
            def _():
                for u in range(2):
                    gu_copy(layer, t + 2, u).start()

        when_chunk(g - 1, e1)

        @pl.loop(0, t_out)
        def _(t):
            down_copy(layer, t).wait()
            slot = lax.rem(t, 3)
            store_part(g, t, jnp.dot(act[...], wb[slot], preferred_element_type=F32))

            @pl.when(t + 3 < t_out)
            def _():
                down_copy(layer, t + 3).start()

    first_copy.start()
    prefetch(0)
    for c in range(CHUNKS):
        hid[c, pl.ds(rows, PAD)] = jnp.zeros((PAD, d_model), BF16)

    @pl.loop(0, n_steps + LAGS)
    def _(g):
        st = lax.div(g, CHUNKS)
        c = lax.rem(g, CHUNKS)
        layer = lax.div(st, 2)
        when_chunk(g - 6, e6)
        when_chunk(g - 5, e5)
        when_chunk(g - 4, e4)
        when_chunk(g - 3, e3)
        when_chunk(g - 2, e2)

        @pl.when(jnp.logical_and(c == 0, jnp.logical_and(st >= 1, st <= n_stage)))
        def _():
            y_sum(st - 1)

        @pl.when(jnp.logical_and(c == 1, jnp.logical_and(st >= 1, st <= n_stage)))
        def _():
            y_done(st - 1)

        cache_events(g)

        @pl.when(jnp.logical_and(g < n_steps, lax.rem(st, 2) == 0))
        def _():
            step_a(g, layer, c)

        @pl.when(jnp.logical_and(g < n_steps, lax.rem(st, 2) == 1))
        def _():
            step_m(g, layer, c)

        @pl.when(g == n_steps)
        def _():
            e1(g - 1)

        @pl.when(g < n_steps)
        def _():
            pair_copy(g).start()

        @pl.when(jnp.logical_and(g < n_steps, c == CHUNKS - 1))
        def _():
            y_pair_copy(st).start()

        @pl.when(g + 1 < n_steps)
        def _():
            prefetch(g + 1)

    tail_copy.wait_send()
    tail_copy.wait_recv()
    tail[...] = tail_in[...]
    for c in range(CHUNKS):
        last_copy(c).wait()


def solution(mesh):
    n_ho, n_tp = mesh.shape['ho'], mesh.shape['tp']
    row_axes = ('pairs', 'ho')
    in_specs = (P('pairs', None, None), P(row_axes, None), P(None, None, 'tp', None, None), P(None, 'tp', None), P(None, None, 'tp'), P(None, None, 'tp'), P(None, 'tp', None), P(None, None), P(None, None))
    out_specs = (P(row_axes, None, None), P(row_axes, None), P(row_axes, None, 'tp', None, None), P(row_axes, None, 'tp', None, None), P(row_axes, None, None, 'tp', None))

    def device_program(prompts, y_first, w_qkv, w_o, w_gate, w_up, w_down, g_attn, g_mlp):
        n_layers, d_model, _, n_slots, head = w_qkv.shape
        n_tok = prompts.shape[1]
        ff = w_gate.shape[2]
        rows = n_tok // CHUNKS
        half = rows // 2
        own = half // (n_tp // 2)
        n_stage = 2 * n_layers
        group = n_slots - 2
        tok_dev = n_tok // n_tp
        wq = jnp.transpose(w_qkv[:, :, 0], (0, 2, 1, 3))
        gains = jnp.stack([g_attn, g_mlp], axis=1).reshape(n_stage, 1, d_model)
        tail_len = d_model + 2 * n_layers * head
        any_spec = pl.BlockSpec(memory_space=pl.ANY)
        vmem_spec = pl.BlockSpec(memory_space=pltpu.VMEM)
        dma = pltpu.SemaphoreType.DMA
        x_last, tail, kv_tok = pl.pallas_call(
            functools.partial(group_kernel, n_ho, n_tp),
            out_shape=(
                jax.ShapeDtypeStruct((n_tok, d_model), BF16),
                jax.ShapeDtypeStruct((1, tail_len), F32),
                jax.ShapeDtypeStruct((n_layers, 2, n_tp, tok_dev, head), BF16),
            ),
            in_specs=[any_spec, vmem_spec, any_spec, any_spec, any_spec, any_spec, any_spec, vmem_spec],
            out_specs=(any_spec, vmem_spec, any_spec),
            scratch_shapes=[
                pltpu.VMEM((CHUNKS, rows + PAD, d_model), BF16),
                pltpu.VMEM((3, rows, d_model), BF16),
                pltpu.VMEM((2, half, d_model), BF16),
                pltpu.VMEM((2, 2, own // 2, d_model), BF16),
                pltpu.VMEM((2, 2, own, d_model), BF16),
                pltpu.VMEM((CHUNKS, own, d_model), BF16),
                pltpu.VMEM((n_layers, 2, n_tok, head), BF16),
                pltpu.VMEM((rows, n_tok), F32),
                pltpu.VMEM((rows + PAD, group * head), BF16),
                pltpu.VMEM((rows + PAD, group * head), BF16),
                pltpu.VMEM((rows + PAD, ff), BF16),
                pltpu.VMEM((rows, d_model), BF16),
                pltpu.VMEM((4, d_model, COLS_A), BF16),
                pltpu.VMEM((3, ff, COLS_B), BF16),
                pltpu.VMEM((n_layers, 2, n_tok, head), BF16),
                pltpu.VMEM((n_layers, 3, 2, 2 * tok_dev, head), BF16),
                pltpu.VMEM((PAD, head), BF16),
                pltpu.VMEM((PAD, head), BF16),
                pltpu.VMEM((1, d_model), F32),
                pltpu.VMEM((n_stage, 1, d_model), F32),
                pltpu.VMEM((n_stage, 1, d_model), F32),
                pltpu.VMEM((n_stage, n_tp // 2, 1, d_model), F32),
                pltpu.VMEM((1, tail_len), F32),
                pltpu.VMEM((1, tail_len), F32),
                dma((4, 2)), dma((3,)), dma, dma((CHUNKS,)),
                dma((2,)), dma((2,)), dma((2,)), dma((2, 2)), dma((2,)), dma((2, 2)),
                dma((2,)), dma((CHUNKS, 2)), dma((2,)), dma((CHUNKS, 2)), dma((4,)), dma((CHUNKS, 4)),
                dma((n_stage,)), dma((n_stage,)), dma((3,)), dma((n_stage, 3)), dma((2,)), dma((2,)),
                dma((n_layers,)), dma((n_layers,)), dma((n_layers, 3)), dma((n_layers, 3)),
                dma((n_layers, 4)), dma((n_layers, 4)), dma((n_layers, 4)),
            ],
            compiler_params=pltpu.CompilerParams(collective_id=0, has_side_effects=True, vmem_limit_bytes=67043328),
            name="group_step",
        )(prompts, y_first.astype(F32), wq, w_o, w_gate, w_up, w_down, gains)
        y_last = tail[:, :d_model]
        kv_new = tail[:, d_model:].reshape(n_layers, 2, 1, head).astype(BF16)
        cache = jnp.transpose(kv_tok, (1, 0, 3, 2, 4))
        return x_last[None], y_last, cache[0][None], cache[1][None], kv_new[None]

    return jax.shard_map(device_program, mesh=mesh, in_specs=in_specs, out_specs=out_specs, check_vma=False)
```

time: 1280 us -> 737 us (0.58)
  Pallas kernels: 0 us -> 710 us
  waiting for transfers between devices: 450 us -> 0 us
  matrix products: 425 us -> 0 us
  blocking collectives: 210 us -> 0 us
  other arithmetic: 136 us -> 2.14 us
  between operations: 17.3 us -> 0.66 us
    pallas_call x0 -> x1, Pallas kernels: none -> 710 us  [device_program(): pl.pallas_call(functools.partial(group_kernel, n_ho, n_tp), out_shape=(ja...]
    psum x4 -> x0, waiting for transfers between devices: 428 us -> none  [the longest x2 215 us: prefill_layer(): x_res = x_res + lax.psum(mlp_part(h_mlp, w_gate, w_up, w_down), 'tp')]
    dot_general x30 -> x0, matrix products: 425 us -> none  [the longest x4 84 us: mlp_part(): gate_pre = jnp.dot(h_mlp, w_gate, preferred_element_type=jnp.float32)]
    reduce_sum x12 -> x0, other arithmetic: 112 us -> none  [the longest x8 66.3 us: rms_norm(): jnp.mean(widened * widened, axis=-1, keepdims=True) + NORM_EPS]
    psum x6 -> x0, blocking collectives: 100 us -> none  [the longest x2 42.2 us: decode_layer(): numer_sum, denom_sum = lax.psum((numer_loc, jnp.sum(p_old, axis=-1)), 'tp')]
    all_to_all x1 -> x0, blocking collectives: 41.8 us -> none  [device_program(): kv_tokens = lax.all_to_all(kv_heads, 'tp', 2, 3, tiled=True)]
    all_gather x2 -> x0, blocking collectives: 37.6 us -> none  [decode_layer(): qkv_all = lax.all_gather(qkv_loc, 'tp', axis=0, tiled=True)]
    pmax x2 -> x0, blocking collectives: 29.8 us -> none  [decode_layer(): top_score = jnp.maximum(lax.pmax(jnp.max(s_old, axis=-1), 'tp'), s_new)]
  transfers between devices with their start and end apart: 5 -> 0, of which waited for: 5 -> 0; matrix products, arithmetic and copies ran while one was open for 6% -> 0% of each run, Pallas kernels for 0% -> 0%
where the time goes in v1:
time: 737 us; the launch traced here: 735 us
  Pallas kernels  710 us (96%)
  local copies, waits for them, and re-layouts  22.4 us (3%)
    pallas_call x1, Pallas kernels, device_program(): pl.pallas_call(functools.partial(group_kernel, n_ho, n_tp), out_shape=(ja...  710 us
    unnamed x3, local copies, waits for them, and re-layouts  17.3 us

profile of v1, /device:TPU:97, one launch (start us, length us, event | category | flops | bytes accessed | tf_op | source)
XLA Modules:
  0.0 735.4 jit_solution(9878960896189318199)
XLA Ops:
  0.6 0.8 pad_maximum_fusion
  1.4 0.1 copy.14
  1.5 0.7 reshape.28.gains
  2.2 1.3 convert_element_type.16.y_first
  3.6 710.2 %group_step.1 = (bf16[2048,4096]{1,0:T(8,128)(2,1)}, f32[1,4608]{1,0:T(1,128)}, bf16[2,2,8,256,128]{4,3,2,1,0:T(8,128)(2,1)}) custom-call(bf16[4,2048,4096]{2,1,0:T(8,128)(2,1)} %prompts.1, f32[1,4096]{1,0:T(1,128)} %convert_element_type.16.y_first, bf16[2,6,4096,128]{3,2,1,0:T(8,128)(2,1)} %bitcast.11, bf16[2,512,4096]{2,1,0:T(8,128)(2,1)} %w_o.1, ...), custom_call_target="tpu_custom_call" | custom-call | tf_op jit(solution)/shard_map/group_step/pallas_call | solution.py:566
  713.8 1.7 fusion.1
  715.5 1.6 copy.15
  717.1 1.6 copy.16
  718.8 1.3 slice.13
  720.1 1.3 fusion
  721.4 14.1 %copy.19 = bf16[1,2048,4096]{2,1,0:T(8,128)(2,1)} copy(bf16[1,2048,4096]{2,1,0:T(8,128)(2,1)} %bitcast.10) | data formatting | bytes 33554432

commit v2 on v1

v2 whole, which is shorter than its diff:
```python
import functools

import jax
import jax.numpy as jnp
from jax import lax
from jax.experimental import pallas as pl
from jax.experimental.pallas import tpu as pltpu
from jax.sharding import PartitionSpec as P

NORM_EPS = 1e-5
MESH = pl.DeviceIdType.MESH
CHUNKS = 8
PAD = 16
COLS_A = 256
COLS_B = 1024
LAGS = 6
NORM_ROWS = 32
VMEM_LIMIT = 187 << 18
CONTRACT_LAST = (((1,), (1,)), ((), ()))
F32 = jnp.float32
BF16 = jnp.bfloat16


def norm_rows(rows_f32, gain):
    inv_rms = lax.rsqrt(jnp.mean(rows_f32 * rows_f32, axis=-1, keepdims=True) + NORM_EPS)
    return (rows_f32 * inv_rms * gain).astype(BF16)


def remote(src, dst, send, recv, device):
    return pltpu.make_async_remote_copy(src_ref=src, dst_ref=dst, send_sem=send, recv_sem=recv, device_id=device, device_id_type=MESH)


def group_kernel(n_ho, n_tp, prompts, y_first, w_qkv, w_o, w_gate, w_up, w_down, g_attn, g_mlp, hid, tail, k_tok, v_tok,
                 part, pair_in, ring1, ring2, resid, kv, scores, qry, att, act, wa, wb, cb0, cb1, relay,
                 k_new, v_new, gains, y_row, y_part, y_pair, y_chip, tail_out, tail_in,
                 wa_sem, wb_sem, in_sem, pair_s, pair_r, r1_s, r1_r, r2_s, r2_r, a1_s, a1_r, a2_s, a2_r, d_s, d_r,
                 yp_s, yp_r, yc_s, yc_r, edge_s, edge_r, c0_s, c0_r, c1_s, c1_r, c2_s, c2_r, c2_l):
    tp = lax.axis_index("tp")
    ho = lax.axis_index("ho")
    n_chip = n_tp // 2
    core = lax.rem(tp, 2)
    chip = lax.div(tp, 2)
    to_right = {"tp": lax.rem(tp + 2, n_tp)}
    to_left = {"tp": lax.rem(tp + n_tp - 2, n_tp)}
    to_far = {"tp": lax.rem(tp + 4, n_tp)}
    to_pair = {"tp": tp + 1 - 2 * core}
    to_up = {"ho": lax.rem(ho + 1, n_ho)}
    to_down = {"ho": lax.rem(ho + n_ho - 1, n_ho)}
    c_right = lax.rem(chip + 1, n_chip)
    c_left = lax.rem(chip + n_chip - 1, n_chip)
    c_far = lax.rem(chip + 2, n_chip)

    n_layers, n_slots, d_model, head = w_qkv.shape
    n_group = n_slots - 2
    ff = w_gate.shape[2]
    n_tok = prompts.shape[1]
    rows = n_tok // CHUNKS
    half = rows // 2
    own = half // n_chip
    sub = own // 2
    all_rows = rows + PAD
    n_stage = 2 * n_layers
    n_steps = n_stage * CHUNKS
    o_rows = n_group * head
    o_per_slot = ff // o_rows
    t_qkv = n_slots * head // COLS_A
    t_gu = ff // COLS_A
    t_out = d_model // COLS_B
    mine = pl.multiple_of(core * half, half)
    theirs = pl.multiple_of(half - core * half, half)
    tok_dev = n_tok // n_tp
    tok_chip = 2 * tok_dev
    scale = head ** -0.5

    def block(base, which):
        return pl.multiple_of(base + which * own, own)

    tail_out[:, pl.ds(0, d_model)] = y_first[...].astype(F32)
    barrier = pltpu.get_barrier_semaphore()
    peers = (to_right, to_left, to_far, to_pair, to_up, to_down)
    for peer in peers:
        pl.semaphore_signal(barrier, inc=1, device_id=peer, device_id_type=MESH)
    def qkv_copy(layer, t, u):
        return pltpu.make_async_copy(w_qkv.at[layer, t * 2 + u], wa.at[t, :, pl.ds(u * head, head)], wa_sem.at[t, u])

    def gu_copy(layer, t, u):
        slot = lax.rem(t, 2) * 2 + u
        cols = pl.ds(pl.multiple_of(t * COLS_A, COLS_A), COLS_A)
        return pltpu.make_async_copy((w_gate, w_up)[u].at[layer, :, cols], wa.at[slot], wa_sem.at[slot, 0])

    def out_tile(t):
        return wb.at[t // o_per_slot, pl.ds((t % o_per_slot) * o_rows, o_rows)]

    def out_copy(layer, t):
        return pltpu.make_async_copy(w_o.at[layer, :, pl.ds(t * COLS_B, COLS_B)], out_tile(t), wb_sem.at[t])

    def down_copy(layer, t):
        slot = lax.rem(t, 2)
        cols = pl.ds(pl.multiple_of(t * COLS_B, COLS_B), COLS_B)
        return pltpu.make_async_copy(w_down.at[layer, :, cols], wb.at[slot], wb_sem.at[slot])

    def prompt_copy(c):
        return pltpu.make_async_copy(prompts.at[ho, pl.ds(pl.multiple_of(c * rows, rows), rows)], hid.at[c, pl.ds(0, rows)], in_sem.at[c])

    def start_qkv(layer):
        for t in range(t_qkv):
            for u in range(2):
                qkv_copy(layer, t, u).start()

    def start_out(layer):
        for t in range(t_out):
            out_copy(layer, t).start()

    def start_gu(layer, t):
        for u in range(2):
            gu_copy(layer, t, u).start()

    def pair_copy(g):
        s = lax.rem(g, 2)
        return remote(part.at[lax.rem(g, 3), pl.ds(theirs, half)], pair_in.at[s], pair_s.at[s], pair_r.at[s], to_pair)

    def r1_copy(g, d):
        s = lax.rem(g, 2)
        base = pl.multiple_of(block(mine, c_far) + d * sub, sub)
        return remote(part.at[lax.rem(g, 3), pl.ds(base, sub)], ring1.at[s, d], r1_s.at[d], r1_r.at[s, d], (to_right, to_left)[d])

    def r2_copy(g, d):
        s = lax.rem(g, 2)
        base = block(mine, (c_right, c_left)[d])
        return remote(part.at[lax.rem(g, 3), pl.ds(base, own)], ring2.at[s, d], r2_s.at[d], r2_r.at[s, d], (to_right, to_left)[d])

    def a1_copy(g, d):
        c = lax.rem(g, CHUNKS)
        ref = hid.at[c, pl.ds(block(mine, chip), own)]
        return remote(ref, ref, a1_s.at[d], a1_r.at[c, d], (to_right, to_left)[d])

    def a2_copy(g, d):
        c = lax.rem(g, CHUNKS)
        base = pl.multiple_of(block(mine, (c_left, c_right)[d]) + d * sub, sub)
        ref = hid.at[c, pl.ds(base, sub)]
        return remote(ref, ref, a2_s.at[d], a2_r.at[c, d], (to_right, to_left)[d])

    def d_copy(g, i):
        c = lax.rem(g, CHUNKS)
        ref = hid.at[c, pl.ds(block(mine, (chip, c_left, c_right, c_far)[i]), own)]
        return remote(ref, ref, d_s.at[i], d_r.at[c, i], to_pair)

    def when_chunk(g, body):
        @pl.when(jnp.logical_and(g >= 0, g < n_steps))
        def _():
            body(g)

    def e1(g):
        pair_copy(g).wait_recv()
        pair_copy(g).wait_send()
        slot = lax.rem(g, 3)
        s = lax.rem(g, 2)

        @pl.loop(0, half // PAD)
        def _(i):
            dst = pl.ds(pl.multiple_of(mine + i * PAD, PAD), PAD)
            src = pl.ds(pl.multiple_of(i * PAD, PAD), PAD)
            part[slot, dst] = (part[slot, dst].astype(F32) + pair_in[s, src].astype(F32)).astype(BF16)

        for d in range(2):
            r1_copy(g, d).start()

    def e2(g):
        slot = lax.rem(g, 3)
        s = lax.rem(g, 2)
        for d in range(2):
            r1_copy(g, d).wait_send()
            r1_copy(g, d).wait_recv()
            dst = pl.ds(pl.multiple_of(block(mine, (c_right, c_left)[d]) + d * sub, sub), sub)
            part[slot, dst] = (part[slot, dst].astype(F32) + ring1[s, d].astype(F32)).astype(BF16)
            r2_copy(g, d).start()

    def e3(g):
        slot = lax.rem(g, 3)
        s = lax.rem(g, 2)
        c = lax.rem(g, CHUNKS)
        st = lax.div(g, CHUNKS)
        for d in range(2):
            r2_copy(g, d).wait_send()
            r2_copy(g, d).wait_recv()
        base = block(mine, chip)

        def new_rows(i):
            loc = pl.ds(i * PAD, PAD)
            dst = pl.ds(pl.multiple_of(base + i * PAD, PAD), PAD)
            total = part[slot, dst].astype(F32) + ring2[s, 0, loc].astype(F32) + ring2[s, 1, loc].astype(F32)
            return loc, dst, (resid[c, loc].astype(F32) + total.astype(BF16).astype(F32)).astype(BF16)

        @pl.when(st < n_stage - 1)
        def _():
            gain = gains[jnp.minimum(st + 1, n_stage - 1)]
            for i in range(own // PAD):
                loc, dst, new = new_rows(i)
                resid[c, loc] = new
                hid[c, dst] = norm_rows(new.astype(F32), gain)

        @pl.when(st == n_stage - 1)
        def _():
            for i in range(own // PAD):
                _, dst, new = new_rows(i)
                hid[c, dst] = new

        for d in range(2):
            a1_copy(g, d).start()
        d_copy(g, 0).start()

    def e4(g):
        for d in range(2):
            a1_copy(g, d).wait_send()
            a1_copy(g, d).wait_recv()
            a2_copy(g, d).start()
        d_copy(g, 0).wait_send()
        d_copy(g, 1).start()
        d_copy(g, 2).start()

    def e5(g):
        for d in range(2):
            a2_copy(g, d).wait_send()
            a2_copy(g, d).wait_recv()
        d_copy(g, 1).wait_send()
        d_copy(g, 2).wait_send()
        d_copy(g, 3).start()

    def e6(g):
        d_copy(g, 3).wait_send()
        for i in range(4):
            d_copy(g, i).wait_recv()

    def y_pair_copy(st):
        return remote(y_part.at[st], y_pair.at[st], yp_s.at[st], yp_r.at[st], to_pair)

    def y_chip_copy(st, i):
        src_chip = chip
        return remote(y_chip.at[st, src_chip], y_chip.at[st, src_chip], yc_s.at[i], yc_r.at[st, i], (to_right, to_left, to_far)[i])

    first_copy = remote(tail_out.at[:, pl.ds(0, d_model)], y_row, edge_s.at[0], edge_r.at[0], to_down)
    tail_copy = remote(tail_out, tail_in, edge_s.at[1], edge_r.at[1], to_up)

    def put_y(gain):
        row = norm_rows(y_row[...], gain)
        hid[CHUNKS - 1, pl.ds(rows, PAD)] = jnp.broadcast_to(row.astype(F32), (PAD, d_model)).astype(BF16)

    def y_sum(st):
        y_pair_copy(st).wait_send()
        y_pair_copy(st).wait_recv()
        y_chip[st, chip] = y_part[st] + y_pair[st]
        for i in range(3):
            y_chip_copy(st, i).start()

    def y_done(st):
        for i in range(3):
            y_chip_copy(st, i).wait_send()
            y_chip_copy(st, i).wait_recv()
        total = y_chip[st, 0]
        for i in range(1, n_chip):
            total = total + y_chip[st, i]
        y_row[...] = y_row[...] + total.astype(BF16).astype(F32)

        @pl.when(st < n_stage - 1)
        def _():
            put_y(gains[jnp.minimum(st + 1, n_stage - 1)])

        @pl.when(st == n_stage - 1)
        def _():
            tail_out[:, pl.ds(0, d_model)] = y_row[...]
            tail_copy.start()

    def c0_copy(layer):
        return remote(kv.at[layer], cb0.at[layer], c0_s.at[layer], c0_r.at[layer], to_up)

    def c1_copy(layer, i):
        def tokens(c):
            return pl.ds(pl.multiple_of(c * tok_chip, tok_chip), tok_chip)

        src, dst, to = (
            (cb0.at[layer, :, tokens(c_right)], cb1.at[layer, 0], to_right),
            (cb0.at[layer, :, tokens(c_left)], cb1.at[layer, 1], to_left),
            (cb0.at[layer, 0, tokens(c_far)], relay.at[layer, 0], to_right),
            (cb0.at[layer, 1, tokens(c_far)], relay.at[layer, 1], to_left),
            (relay.at[layer, 0], cb1.at[layer, 2, 0], to_right),
            (relay.at[layer, 1], cb1.at[layer, 2, 1], to_left),
        )[i]
        return remote(src, dst, c1_s.at[layer, i], c1_r.at[layer, i], to)

    def c2_source(layer, i, n, which):
        off = pl.multiple_of(which * tok_dev, tok_dev)
        if i < 3:
            return cb1.at[layer, i, n, pl.ds(off, tok_dev)], (c_left, c_right, c_far)[i]
        return cb0.at[layer, n, pl.ds(pl.multiple_of(chip * tok_chip + off, tok_dev), tok_dev)], chip

    def c2_copy(layer, i, n):
        src, src_chip = c2_source(layer, i, n, 1 - core)
        return remote(src, (k_tok, v_tok)[n].at[layer, 2 * src_chip + core], c2_s.at[layer, i, n], c2_r.at[layer, i, n], to_pair)

    def c2_local(layer, i, n):
        src, src_chip = c2_source(layer, i, n, core)
        return pltpu.make_async_copy(src, (k_tok, v_tok)[n].at[layer, 2 * src_chip + core], c2_l.at[layer, i, n])

    def cache_events(g):
        for layer in range(n_layers):
            at = (2 * layer + 1) * CHUNKS

            @pl.when(g == at)
            def _():
                c0_copy(layer).start()

            @pl.when(g == at + 2)
            def _():
                c0_copy(layer).wait_send()
                c0_copy(layer).wait_recv()
                c1_copy(layer, 0).start()
                c1_copy(layer, 1).start()

            @pl.when(g == at + 3)
            def _():
                c1_copy(layer, 2).start()
                c1_copy(layer, 3).start()

            @pl.when(g == at + 5)
            def _():
                for i in (2, 3):
                    c1_copy(layer, i).wait_send()
                    c1_copy(layer, i).wait_recv()
                for i in (4, 5):
                    c1_copy(layer, i).start()

            @pl.when(g == at + 7)
            def _():
                for i in (0, 1, 4, 5):
                    c1_copy(layer, i).wait_send()
                    c1_copy(layer, i).wait_recv()
                for i in range(4):
                    for n in range(2):
                        c2_copy(layer, i, n).start()
                        c2_local(layer, i, n).start()

            @pl.when(g == at + 9)
            def _():
                for i in range(4):
                    for n in range(2):
                        c2_copy(layer, i, n).wait_send()
                        c2_copy(layer, i, n).wait_recv()
                        c2_local(layer, i, n).wait()

    def store_part(g, t, acc):
        cols = pl.ds(pl.multiple_of(t * COLS_B, COLS_B), COLS_B)
        part[lax.rem(g, 3), :, cols] = acc[:rows].astype(BF16)
        y_part[lax.div(g, CHUNKS), :, cols] = acc[rows:rows + 1]

    def first_norm(c):
        prompt_copy(c).wait()
        gain = gains[0]
        for i in range(own // PAD):
            resid[c, pl.ds(i * PAD, PAD)] = hid[c, pl.ds(pl.multiple_of(block(mine, chip) + i * PAD, PAD), PAD)]

        @pl.loop(0, rows // NORM_ROWS)
        def _(i):
            loc = pl.ds(pl.multiple_of(i * NORM_ROWS, NORM_ROWS), NORM_ROWS)
            hid[c, loc] = norm_rows(hid[c, loc].astype(F32), gain)

        @pl.when(c == CHUNKS - 1)
        def _():
            first_copy.wait_send()
            first_copy.wait_recv()
            put_y(gain)

    def attention(layer, c):
        causal = lax.broadcasted_iota(jnp.int32, (rows, rows), 0) >= lax.broadcasted_iota(jnp.int32, (rows, rows), 1)
        heads = range(n_group)

        def loc_of(j):
            return pl.ds(pl.multiple_of(j * rows, rows), rows)

        def score(h, loc):
            q = qry[pl.ds(0, rows), pl.ds(h * head, head)]
            return lax.dot_general(q, kv[layer, 0, loc], CONTRACT_LAST, preferred_element_type=F32) * scale

        def fold(op, x, s):
            for b in range(rows // head):
                x = op(x, s[:, b * head:(b + 1) * head])
            return x

        def first(j, tops):
            loc = loc_of(j)
            new = []
            for h in heads:
                s = score(h, loc)
                scores[h, :, loc] = s
                new.append(fold(jnp.maximum, tops[h], s))
            return tuple(new)

        lowest = jnp.full((rows, head), -jnp.inf, F32)
        tops = lax.fori_loop(0, c, first, tuple(lowest for _ in heads))
        diag = loc_of(c)
        row_top = []
        for h in heads:
            s = jnp.where(causal, score(h, diag), -jnp.inf)
            scores[h, :, diag] = s
            row_top.append(jnp.max(fold(jnp.maximum, tops[h], s), axis=1, keepdims=True))

        def second(j, carry):
            loc = loc_of(j)
            new = []
            for h in heads:
                denom, numer = carry[h]
                p = jnp.exp(scores[h, :, loc] - row_top[h])
                new.append((fold(jnp.add, denom, p), numer + jnp.dot(p.astype(BF16), kv[layer, 1, loc], preferred_element_type=F32)))
            return tuple(new)

        zero = jnp.zeros((rows, head), F32)
        sums = lax.fori_loop(0, c + 1, second, tuple((zero, zero) for _ in heads))
        for h in heads:
            denom, numer = sums[h]
            att[pl.ds(0, rows), pl.ds(h * head, head)] = (numer / jnp.sum(denom, axis=1, keepdims=True)).astype(BF16)

    def attention_new(layer):
        q = jnp.concatenate([qry[pl.ds(rows, PAD), pl.ds(h * head, head)] for h in range(n_group)], axis=0)
        k_row = k_new[...].astype(F32)[:1]
        v_row = v_new[...].astype(F32)[:1]
        s_new = jnp.sum(q.astype(F32) * k_row, axis=1, keepdims=True) * scale
        s_old = lax.dot_general(q, kv[layer, 0], CONTRACT_LAST, preferred_element_type=F32) * scale
        top = jnp.maximum(jnp.max(s_old, axis=1, keepdims=True), s_new)
        p_old = jnp.exp(s_old - top)
        p_new = jnp.exp(s_new - top)
        denom = jnp.sum(p_old, axis=1, keepdims=True) + p_new
        numer = jnp.dot(p_old.astype(BF16), kv[layer, 1], preferred_element_type=F32) + p_new * v_row
        out = (numer / denom).astype(BF16)
        for h in range(n_group):
            att[pl.ds(rows, PAD), pl.ds(h * head, head)] = out[h * PAD:(h + 1) * PAD]

    def step_a(g, layer, c):
        @pl.when(layer == 0)
        def _():
            first_norm(c)

        @pl.when(c == 0)
        def _():
            for t in range(t_qkv):
                for u in range(2):
                    qkv_copy(layer, t, u).wait()

        for t in range(t_qkv):
            out = jnp.dot(hid[c], wa[t], preferred_element_type=F32).astype(BF16)
            if t < t_qkv - 1:
                qry[:, pl.ds(t * COLS_A, COLS_A)] = out
            else:
                loc = pl.ds(pl.multiple_of(c * rows, rows), rows)
                kv[layer, 0, loc] = out[:rows, :head]
                kv[layer, 1, loc] = out[:rows, head:]
                k_new[...] = out[rows:, :head]
                v_new[...] = out[rows:, head:]

        @pl.when(c == CHUNKS - 1)
        def _():
            for t in range(2):
                start_gu(layer, t)

        when_chunk(g - 1, e1)
        attention(layer, c)

        @pl.when(c == CHUNKS - 1)
        def _():
            attention_new(layer)
            for ll in range(n_layers):
                @pl.when(layer == ll)
                def _():
                    tail_out[:, pl.ds(d_model + 2 * ll * head, head)] = k_new[...].astype(F32)[:1]
                    tail_out[:, pl.ds(d_model + (2 * ll + 1) * head, head)] = v_new[...].astype(F32)[:1]

        @pl.when(c == 0)
        def _():
            for t in range(t_out):
                out_copy(layer, t).wait()

        for t in range(t_out):
            store_part(g, t, jnp.dot(att[...], out_tile(t)[...], preferred_element_type=F32))

        @pl.when(c == CHUNKS - 1)
        def _():
            for t in range(2):
                down_copy(layer, t).start()

    def step_m(g, layer, c):
        @pl.loop(0, t_gu)
        def _(t):
            for u in range(2):
                gu_copy(layer, t, u).wait()
            slot = lax.rem(t, 2) * 2
            gate = jnp.dot(hid[c], wa[slot], preferred_element_type=F32)
            up = jnp.dot(hid[c], wa[slot + 1], preferred_element_type=F32)
            act[:, pl.ds(pl.multiple_of(t * COLS_A, COLS_A), COLS_A)] = (jax.nn.silu(gate) * up).astype(BF16)

            @pl.when(jnp.logical_or(t + 2 < t_gu, c + 1 < CHUNKS))
            def _():
                start_gu(layer, lax.rem(t + 2, t_gu))

        @pl.when(jnp.logical_and(c == CHUNKS - 1, layer + 1 < n_layers))
        def _():
            start_qkv(jnp.minimum(layer + 1, n_layers - 1))

        when_chunk(g - 1, e1)

        @pl.loop(0, t_out)
        def _(t):
            down_copy(layer, t).wait()
            store_part(g, t, jnp.dot(act[...], wb[lax.rem(t, 2)], preferred_element_type=F32))

            @pl.when(jnp.logical_or(t + 2 < t_out, c + 1 < CHUNKS))
            def _():
                down_copy(layer, lax.rem(t + 2, t_out)).start()

        @pl.when(jnp.logical_and(c == CHUNKS - 1, layer + 1 < n_layers))
        def _():
            start_out(jnp.minimum(layer + 1, n_layers - 1))

    start_qkv(0)
    prompt_copy(0).start()
    start_out(0)
    for c in range(1, CHUNKS):
        prompt_copy(c).start()
    for layer in range(n_layers):
        gains[2 * layer] = g_attn[layer:layer + 1]
        gains[2 * layer + 1] = g_mlp[layer:layer + 1]
    for c in range(CHUNKS):
        hid[c, pl.ds(rows, PAD)] = jnp.zeros((PAD, d_model), BF16)
    att[pl.ds(rows, PAD)] = jnp.zeros((PAD, o_rows), BF16)
    pl.semaphore_wait(barrier, len(peers))
    first_copy.start()

    @pl.loop(0, n_steps + LAGS)
    def _(g):
        st = lax.div(g, CHUNKS)
        c = lax.rem(g, CHUNKS)
        layer = lax.div(st, 2)
        when_chunk(g - 6, e6)
        when_chunk(g - 5, e5)
        when_chunk(g - 4, e4)
        when_chunk(g - 3, e3)
        when_chunk(g - 2, e2)

        @pl.when(jnp.logical_and(c == 0, jnp.logical_and(st >= 1, st <= n_stage)))
        def _():
            y_sum(st - 1)

        @pl.when(jnp.logical_and(c == 1, jnp.logical_and(st >= 1, st <= n_stage)))
        def _():
            y_done(st - 1)

        cache_events(g)

        @pl.when(jnp.logical_and(g < n_steps, lax.rem(st, 2) == 0))
        def _():
            step_a(g, layer, c)

        @pl.when(jnp.logical_and(g < n_steps, lax.rem(st, 2) == 1))
        def _():
            step_m(g, layer, c)

        @pl.when(g == n_steps)
        def _():
            e1(g - 1)

        @pl.when(g < n_steps)
        def _():
            pair_copy(g).start()

        @pl.when(jnp.logical_and(g < n_steps, c == CHUNKS - 1))
        def _():
            y_pair_copy(st).start()

    tail_copy.wait_send()
    tail_copy.wait_recv()
    tail[...] = tail_in[...]


def solution(mesh):
    n_ho, n_tp = mesh.shape['ho'], mesh.shape['tp']
    row_axes = ('pairs', 'ho')
    in_specs = (P('pairs', None, None), P(row_axes, None), P(None, None, 'tp', None, None), P(None, 'tp', None), P(None, None, 'tp'), P(None, None, 'tp'), P(None, 'tp', None), P(None, None), P(None, None))
    out_specs = (P(row_axes, None, None), P(row_axes, None), P(row_axes, None, 'tp', None, None), P(row_axes, None, 'tp', None, None), P(row_axes, None, None, 'tp', None))

    def device_program(prompts, y_first, w_qkv, w_o, w_gate, w_up, w_down, g_attn, g_mlp):
        n_layers, d_model, _, n_slots, head = w_qkv.shape
        n_tok = prompts.shape[1]
        ff = w_gate.shape[2]
        rows = n_tok // CHUNKS
        half = rows // 2
        own = half // (n_tp // 2)
        n_stage = 2 * n_layers
        group = n_slots - 2
        tok_dev = n_tok // n_tp
        wq = jnp.transpose(w_qkv[:, :, 0], (0, 2, 1, 3))
        tail_len = d_model + 2 * n_layers * head
        any_spec = pl.BlockSpec(memory_space=pl.ANY)
        vmem_spec = pl.BlockSpec(memory_space=pltpu.VMEM)
        dma = pltpu.SemaphoreType.DMA
        hid, tail, k_tok, v_tok = pl.pallas_call(
            functools.partial(group_kernel, n_ho, n_tp),
            out_shape=(
                pltpu.VMEM((CHUNKS, rows + PAD, d_model), BF16),
                jax.ShapeDtypeStruct((1, tail_len), F32),
                jax.ShapeDtypeStruct((n_layers, n_tp, tok_dev, head), BF16),
                jax.ShapeDtypeStruct((n_layers, n_tp, tok_dev, head), BF16),
            ),
            in_specs=[any_spec, vmem_spec, any_spec, any_spec, any_spec, any_spec, any_spec, vmem_spec, vmem_spec],
            out_specs=(vmem_spec, vmem_spec, any_spec, any_spec),
            scratch_shapes=[
                pltpu.VMEM((3, rows, d_model), BF16),
                pltpu.VMEM((2, half, d_model), BF16),
                pltpu.VMEM((2, 2, own // 2, d_model), BF16),
                pltpu.VMEM((2, 2, own, d_model), BF16),
                pltpu.VMEM((CHUNKS, own, d_model), BF16),
                pltpu.VMEM((n_layers, 2, n_tok, head), BF16),
                pltpu.VMEM((group, rows, n_tok), F32),
                pltpu.VMEM((rows + PAD, group * head), BF16),
                pltpu.VMEM((rows + PAD, group * head), BF16),
                pltpu.VMEM((rows + PAD, ff), BF16),
                pltpu.VMEM((4, d_model, COLS_A), BF16),
                pltpu.VMEM((2, ff, COLS_B), BF16),
                pltpu.VMEM((n_layers, 2, n_tok, head), BF16),
                pltpu.VMEM((n_layers, 3, 2, 2 * tok_dev, head), BF16),
                pltpu.VMEM((n_layers, 2, 2 * tok_dev, head), BF16),
                pltpu.VMEM((PAD, head), BF16),
                pltpu.VMEM((PAD, head), BF16),
                pltpu.VMEM((n_stage, 1, d_model), F32),
                pltpu.VMEM((1, d_model), F32),
                pltpu.VMEM((n_stage, 1, d_model), F32),
                pltpu.VMEM((n_stage, 1, d_model), F32),
                pltpu.VMEM((n_stage, n_tp // 2, 1, d_model), F32),
                pltpu.VMEM((1, tail_len), F32),
                pltpu.VMEM((1, tail_len), F32),
                dma((4, 2)), dma((d_model // COLS_B,)), dma((CHUNKS,)),
                dma((2,)), dma((2,)), dma((2,)), dma((2, 2)), dma((2,)), dma((2, 2)),
                dma((2,)), dma((CHUNKS, 2)), dma((2,)), dma((CHUNKS, 2)), dma((4,)), dma((CHUNKS, 4)),
                dma((n_stage,)), dma((n_stage,)), dma((3,)), dma((n_stage, 3)), dma((2,)), dma((2,)),
                dma((n_layers,)), dma((n_layers,)), dma((n_layers, 6)), dma((n_layers, 6)),
                dma((n_layers, 4, 2)), dma((n_layers, 4, 2)), dma((n_layers, 4, 2)),
            ],
            compiler_params=pltpu.CompilerParams(collective_id=0, has_side_effects=True, vmem_limit_bytes=VMEM_LIMIT),
            name="group_step",
        )(prompts, y_first, wq, w_o, w_gate, w_up, w_down, g_attn, g_mlp)
        y_last = tail[:, :d_model]
        kv_new = tail[:, d_model:].reshape(n_layers, 2, 1, head).astype(BF16)
        x_last = hid[:, :rows].reshape(n_tok, d_model)
        k_cache, v_cache = jnp.swapaxes(k_tok, 1, 2), jnp.swapaxes(v_tok, 1, 2)
        return x_last[None], y_last, k_cache[None], v_cache[None], kv_new[None]

    return jax.shard_map(device_program, mesh=mesh, in_specs=in_specs, out_specs=out_specs, check_vma=False)
```

time: 737 us -> 612 us (0.83)
  Pallas kernels: 710 us -> 598 us
  local copies, waits for them, and re-layouts: 22.4 us -> 12.9 us
    pallas_call x1, Pallas kernels: 710 us -> 598 us  [device_program(): pl.pallas_call(functools.partial(group_kernel, n_ho, n_tp), out_shape=(pl...]
    unnamed x3 -> x6, local copies, waits for them, and re-layouts: 17.3 us -> 3.31 us
where the time goes in v2:
time: 612 us
  Pallas kernels  598 us (98%)
  local copies, waits for them, and re-layouts  12.9 us (2%)
    pallas_call x1, Pallas kernels, device_program(): pl.pallas_call(functools.partial(group_kernel, n_ho, n_tp), out_shape=(pl...  598 us

profile of v2, /device:TPU:97, one launch (start us, length us, event | category | flops | bytes accessed | tf_op | source)
XLA Modules:
  0.0 611.8 jit_solution(5657449061690479640)
XLA Ops:
  0.6 598.3 %group_step.1 = (bf16[8,272,4096]{2,1,0:T(8,128)(2,1)S(1)}, f32[1,4608]{1,0:T(1,128)}, bf16[2,8,256,128]{3,2,1,0:T(8,128)(2,1)}, bf16[2,8,256,128]{3,2,1,0:T(8,128)(2,1)}) custom-call(bf16[4,2048,4096]{2,1,0:T(8,128)(2,1)} %prompts.1, bf16[1,4096]{1,0:T(2,128)(2,1)} %y_first.1, bf16[2,6,4096,128]{3,2,1,0:T(8,128)(2,1)} %bitcast.14, ...), custom_call_target="tpu_custom_call" | custom-call | tf_op jit(solution)/shard_map/group_step/pallas_call | solution.py:602
  598.9 0.0 copy-start.1
  599.0 0.0 copy-start
  599.0 1.5 slice.11
  600.4 1.3 fusion
  601.7 6.8 %slice.10 = bf16[8,256,4096]{2,1,0:T(8,128)(2,1)} slice(bf16[8,272,4096]{2,1,0:T(8,128)(2,1)S(1)} %get-tuple-element.9), slice={[0:8], [0:256], [0:4096]} | slice | bytes 33554432 | tf_op jit(solution)/shard_map/slice | solution.py:649
  608.5 0.0 copy-done.1
  608.5 1.6 copy.14
  610.2 0.0 copy-done
  610.2 1.6 copy.15
Async XLA Ops:
  598.9 9.6 %copy-start.1 = (bf16[2,8,256,128]{3,2,1,0:T(8,128)(2,1)S(1)}, bf16[2,8,256,128]{3,2,1,0:T(8,128)(2,1)}, u32[]{:S(2)}) copy-start(bf16[2,8,256,128]{3,2,1,0:T(8,128)(2,1)} %get-tuple-element.11) | copy-start | bytes 3145732
  599.0 11.2 %copy-start = (bf16[2,8,256,128]{3,2,1,0:T(8,128)(2,1)S(1)}, bf16[2,8,256,128]{3,2,1,0:T(8,128)(2,1)}, u32[]{:S(2)}) copy-start(bf16[2,8,256,128]{3,2,1,0:T(8,128)(2,1)} %get-tuple-element.12) | copy-start | bytes 3145732

commit v3 on v2

v3 whole, which is shorter than its diff:
```python
import functools

import jax
import jax.numpy as jnp
from jax import lax
from jax.experimental import pallas as pl
from jax.experimental.pallas import tpu as pltpu
from jax.sharding import PartitionSpec as P

NORM_EPS = 1e-5
MESH = pl.DeviceIdType.MESH
CHUNKS = 8
PAD = 16
COLS_A = 256
COLS_B = 1024
LAGS = 6
NORM_ROWS = 32
VMEM_LIMIT = 46 << 20
WX_STEPS = (0, 0, 1, 2, 10, 11, 11, 12, 12, 13)
CACHE_STEPS = ((8, 16, 18, 20, 22, 24), (24, 26, 27, 29, 31, 33))
SLOTS_B = 3
CONTRACT_LAST = (((1,), (1,)), ((), ()))
F32 = jnp.float32
BF16 = jnp.bfloat16


def norm_rows(rows_f32, gain):
    inv_rms = lax.rsqrt(jnp.mean(rows_f32 * rows_f32, axis=-1, keepdims=True) + NORM_EPS)
    return (rows_f32 * inv_rms * gain).astype(BF16)


def remote(src, dst, send, recv, device):
    return pltpu.make_async_remote_copy(src_ref=src, dst_ref=dst, send_sem=send, recv_sem=recv, device_id=device, device_id_type=MESH)


def chip_group(chip):
    return lax.rem(lax.div(chip + 1, 2) + 1, 2)


def chip_member(chip):
    return lax.div(chip, 2)


def group_kernel(n_ho, n_tp, prompts, y_first, w_qkv, w_o, w_gate, w_up, w_down, g_attn, g_mlp, hid, tail, k_tok, v_tok, wq_x, wo_x, cb0, cb1, relay,
                 part, pair_in, ring1, ring2, resid, kv0, kv1, scores, qry, qry_new, att0, att1, act, wa, wb,
                 k_new, v_new, gains, y_row, y_part, y_pair, y_chip, tail_out, tail_in,
                 wa_sem, wb_sem, in_sem, pair_s, pair_r, r1_s, r1_r, r2_s, r2_r, a1_s, a1_r, a2_s, a2_r, d_s, d_r,
                 yp_s, yp_r, yc_s, yc_r, edge_s, edge_r, c0_s, c0_r, c1_s, c1_r, c2_s, c2_r, c2_l, kx_s, kx_r, wx_s, wx_r, wy_s, wy_r):
    tp = lax.axis_index("tp")
    ho = lax.axis_index("ho")
    n_chip = n_tp // 2
    core = lax.rem(tp, 2)
    chip = lax.div(tp, 2)
    odd = lax.rem(chip, 2)
    to_right = {"tp": lax.rem(tp + 2, n_tp)}
    to_left = {"tp": lax.rem(tp + n_tp - 2, n_tp)}
    to_far = {"tp": lax.rem(tp + 4, n_tp)}
    to_pair = {"tp": tp + 1 - 2 * core}
    to_up = {"ho": lax.rem(ho + 1, n_ho)}
    to_down = {"ho": lax.rem(ho + n_ho - 1, n_ho)}
    c_right = lax.rem(chip + 1, n_chip)
    c_left = lax.rem(chip + n_chip - 1, n_chip)
    c_far = lax.rem(chip + 2, n_chip)
    c_mate = lax.rem(chip + n_chip + 2 * odd - 1, n_chip)
    to_mate = {"tp": lax.rem(tp + n_tp + 4 * odd - 2, n_tp)}
    to_swap = {"tp": lax.rem(tp + n_tp + 2 - 4 * odd, n_tp)}
    mate_out = 1 - odd
    mate_in = odd
    grp = chip_group(chip)

    n_layers, n_slots, d_model, head = w_qkv.shape
    n_group = n_slots - 2
    ff = w_gate.shape[2]
    n_tok = prompts.shape[1]
    rows = n_tok // CHUNKS
    half = rows // 2
    seg = half // 2
    own = half // n_chip
    sub = own // 2
    n_stage = 2 * n_layers
    n_steps = n_stage * CHUNKS
    swap_stage = n_stage - 2
    swap_layer = n_layers - 1
    o_rows = n_group * head
    o_per_slot = ff // o_rows
    t_qkv = n_slots * head // COLS_A
    t_gu = ff // COLS_A
    t_out = d_model // COLS_B
    tok_dev = n_tok // n_tp
    tok_chip = 2 * tok_dev
    scale = head ** -0.5

    def block_row(c, k):
        return pl.multiple_of(chip_group(c) * half + k * seg + chip_member(c) * own, own)

    def part_block(g, c, first, size):
        return part.at[lax.rem(g, 3), chip_group(c), core, pl.ds(pl.multiple_of(chip_member(c) * own + first, size), size)]

    tail_out[:, pl.ds(0, d_model)] = y_first[...].astype(F32)
    barrier = pltpu.get_barrier_semaphore()
    peers = (to_right, to_left, to_far, to_pair, to_up, to_down)
    for peer in peers:
        pl.semaphore_signal(barrier, inc=1, device_id=peer, device_id_type=MESH)

    def qkv_copy(layer, t, u):
        return pltpu.make_async_copy(w_qkv.at[layer, t * 2 + u], wa.at[t, :, pl.ds(u * head, head)], wa_sem.at[t, u])

    def swap_qkv_copy(slot, t, u):
        src = w_qkv.at[swap_layer, t * 2 + u] if t < t_qkv else wq_x.at[(t - t_qkv) * 2 + u]
        return pltpu.make_async_copy(src, wa.at[slot, :, pl.ds(u * head, head)], wa_sem.at[slot, u])

    def start_swap_qkv(c, pair):
        slot = lax.rem(c * t_qkv + pair, 2) * 2
        for v in range(2):
            for u in range(2):
                swap_qkv_copy(slot + v, 2 * pair + v, u).start()

    def gu_copy(layer, t, u):
        slot = lax.rem(t, 2) * 2 + u
        cols = pl.ds(pl.multiple_of(t * COLS_A, COLS_A), COLS_A)
        return pltpu.make_async_copy((w_gate, w_up)[u].at[layer, :, cols], wa.at[slot], wa_sem.at[slot, 0])

    def out_tile(t):
        return wb.at[t // o_per_slot, pl.ds((t % o_per_slot) * o_rows, o_rows)]

    def out_copy(layer, t):
        return pltpu.make_async_copy(w_o.at[layer, :, pl.ds(t * COLS_B, COLS_B)], out_tile(t), wb_sem.at[t])

    def swap_out_copy(c, t, v):
        slot = lax.rem(c * t_out + t, SLOTS_B)
        src = (w_o.at[swap_layer], wo_x)[v].at[:, pl.ds(t * COLS_B, COLS_B)]
        return pltpu.make_async_copy(src, wb.at[slot, pl.ds(v * o_rows, o_rows)], wb_sem.at[slot * 2 + v])

    def down_copy(layer, c, t):
        slot = lax.rem(c * t_out + t, SLOTS_B)
        cols = pl.ds(pl.multiple_of(t * COLS_B, COLS_B), COLS_B)
        return pltpu.make_async_copy(w_down.at[layer, :, cols], wb.at[slot], wb_sem.at[slot])

    def prompt_copy(c):
        return pltpu.make_async_copy(prompts.at[ho, pl.ds(pl.multiple_of(c * rows, rows), rows)], hid.at[c, pl.ds(0, rows)], in_sem.at[c])

    def start_gu(layer, t):
        for u in range(2):
            gu_copy(layer, t, u).start()

    for t in range(t_qkv):
        for u in range(2):
            qkv_copy(0, t, u).start()
    prompt_copy(0).start()
    for t in range(t_out):
        out_copy(0, t).start()
    for c in range(1, CHUNKS):
        prompt_copy(c).start()

    def pair_copy(g):
        s = lax.rem(g, 2)
        return remote(part.at[lax.rem(g, 3), :, 1 - core], pair_in.at[s], pair_s.at[s], pair_r.at[s], to_pair)

    def half_pair_copy(g):
        s = lax.rem(g, 2)
        return remote(part.at[lax.rem(g, 3), grp, 1 - core], pair_in.at[s, grp], pair_s.at[s], pair_r.at[s], to_pair)

    def r1_copy(g, d):
        s = lax.rem(g, 2)
        return remote(part_block(g, c_far, d * sub, sub), ring1.at[s, d], r1_s.at[d], r1_r.at[s, d], (to_right, to_left)[d])

    def r2_copy(g, d):
        s = lax.rem(g, 2)
        return remote(part_block(g, (c_right, c_left)[d], 0, own), ring2.at[s, d], r2_s.at[d], r2_r.at[s, d], (to_right, to_left)[d])

    def r2_mate(g, d):
        s = lax.rem(g, 2)
        return remote(part_block(g, c_mate, 0, own), ring2.at[s, d], r2_s.at[d], r2_r.at[s, d], to_mate)

    def a1_copy(g, d):
        c = lax.rem(g, CHUNKS)
        ref = hid.at[c, pl.ds(block_row(chip, core), own)]
        return remote(ref, ref, a1_s.at[d], a1_r.at[c, d], (to_right, to_left)[d])

    def a1_mate(g, d):
        c = lax.rem(g, CHUNKS)
        ref = hid.at[c, pl.ds(block_row(chip, core), own)]
        return remote(ref, ref, a1_s.at[d], a1_r.at[c, d], to_mate)

    def a2_copy(g, d):
        c = lax.rem(g, CHUNKS)
        base = pl.multiple_of(block_row((c_left, c_right)[d], core) + d * sub, sub)
        ref = hid.at[c, pl.ds(base, sub)]
        return remote(ref, ref, a2_s.at[d], a2_r.at[c, d], (to_right, to_left)[d])

    def d_copy(g, i, of=None):
        c = lax.rem(g, CHUNKS)
        ref = hid.at[c, pl.ds(block_row((chip, c_left, c_right, c_far)[i] if of is None else of, core), own)]
        return remote(ref, ref, d_s.at[i], d_r.at[c, i], to_pair)

    def by_stage(g, stage, then, other):
        is_it = lax.div(g, CHUNKS) == stage

        @pl.when(is_it)
        def _():
            then()

        @pl.when(jnp.logical_not(is_it))
        def _():
            other()

    def when_chunk(g, body):
        @pl.when(jnp.logical_and(g >= 0, g < n_steps))
        def _():
            body(g)

    def add_pair(g, gi):
        slot = lax.rem(g, 3)
        s = lax.rem(g, 2)

        @pl.loop(0, seg // PAD)
        def _(i):
            loc = pl.ds(pl.multiple_of(i * PAD, PAD), PAD)
            part[slot, gi, core, loc] = (part[slot, gi, core, loc].astype(F32) + pair_in[s, gi, loc].astype(F32)).astype(BF16)

    def e0(g):
        by_stage(g, swap_stage, lambda: half_pair_copy(g).start(), lambda: pair_copy(g).start())

    def e1(g):
        def swapped():
            half_pair_copy(g).wait_recv()
            half_pair_copy(g).wait_send()
            add_pair(g, grp)

        def usual():
            pair_copy(g).wait_recv()
            pair_copy(g).wait_send()
            for gi in range(2):
                add_pair(g, gi)
            for d in range(2):
                r1_copy(g, d).start()

        by_stage(g, swap_stage, swapped, usual)

    def e2(g):
        def usual():
            s = lax.rem(g, 2)
            for d in range(2):
                r1_copy(g, d).wait_send()
                r1_copy(g, d).wait_recv()
            for d in range(2):
                ref = part_block(g, (c_right, c_left)[d], d * sub, sub)
                ref[...] = (ref[...].astype(F32) + ring1[s, d].astype(F32)).astype(BF16)
                r2_copy(g, d).start()

        by_stage(g, swap_stage, lambda: r2_mate(g, mate_out).start(), usual)

    def e3(g):
        s = lax.rem(g, 2)
        c = lax.rem(g, CHUNKS)
        st = lax.div(g, CHUNKS)
        mine = part_block(g, chip, 0, own)
        base = block_row(chip, core)

        def finish(totals):
            def new_rows(i):
                loc = pl.ds(i * PAD, PAD)
                dst = pl.ds(pl.multiple_of(base + i * PAD, PAD), PAD)
                total = mine[loc].astype(F32)
                for d in totals:
                    total = total + ring2[s, d, loc].astype(F32)
                return loc, dst, (resid[c, loc].astype(F32) + total.astype(BF16).astype(F32)).astype(BF16)

            @pl.when(st < n_stage - 1)
            def _():
                gain = gains[jnp.minimum(st + 1, n_stage - 1)]
                for i in range(own // PAD):
                    loc, dst, new = new_rows(i)
                    resid[c, loc] = new
                    hid[c, dst] = norm_rows(new.astype(F32), gain)

            @pl.when(st == n_stage - 1)
            def _():
                for i in range(own // PAD):
                    _, dst, new = new_rows(i)
                    hid[c, dst] = new

        def swapped():
            r2_mate(g, mate_out).wait_send()
            r2_mate(g, mate_in).wait_recv()
            finish((mate_in,))

        def usual():
            for d in range(2):
                r2_copy(g, d).wait_send()
                r2_copy(g, d).wait_recv()
            finish((0, 1))

        by_stage(g, swap_stage, swapped, usual)

        def to_both():
            for d in range(2):
                a1_copy(g, d).start()

        by_stage(g, swap_stage - 1, lambda: a1_mate(g, mate_out).start(), to_both)
        d_copy(g, 0).start()

    def e4(g):
        def swapped():
            a1_mate(g, mate_out).wait_send()
            a1_mate(g, mate_in).wait_recv()
            d_copy(g, 0).wait_send()
            d_copy(g, 1, c_mate).start()

        def usual():
            for d in range(2):
                a1_copy(g, d).wait_send()
                a1_copy(g, d).wait_recv()
                a2_copy(g, d).start()
            d_copy(g, 0).wait_send()
            d_copy(g, 1).start()
            d_copy(g, 2).start()

        by_stage(g, swap_stage - 1, swapped, usual)

    def e5(g):
        def usual():
            for d in range(2):
                a2_copy(g, d).wait_send()
                a2_copy(g, d).wait_recv()
            d_copy(g, 1).wait_send()
            d_copy(g, 2).wait_send()
            d_copy(g, 3).start()

        by_stage(g, swap_stage - 1, lambda: d_copy(g, 1, c_mate).wait_send(), usual)

    def e6(g):
        def swapped():
            for i in range(2):
                d_copy(g, i).wait_recv()

        def usual():
            d_copy(g, 3).wait_send()
            for i in range(4):
                d_copy(g, i).wait_recv()

        by_stage(g, swap_stage - 1, swapped, usual)

    def y_pair_copy(st):
        return remote(y_part.at[st], y_pair.at[st], yp_s.at[st], yp_r.at[st], to_pair)

    def y_chip_copy(st, i):
        return remote(y_chip.at[st, chip], y_chip.at[st, chip], yc_s.at[i], yc_r.at[st, i], (to_right, to_left, to_far)[i])

    first_copy = remote(tail_out.at[:, pl.ds(0, d_model)], y_row, edge_s.at[0], edge_r.at[0], to_down)
    tail_copy = remote(tail_out, tail_in, edge_s.at[1], edge_r.at[1], to_up)

    def put_y(gain, at):
        row = norm_rows(y_row[...], gain)
        hid[CHUNKS - 1, pl.ds(at, PAD)] = jnp.broadcast_to(row.astype(F32), (PAD, d_model)).astype(BF16)

    def y_sum(st):
        y_pair_copy(st).wait_send()
        y_pair_copy(st).wait_recv()
        y_chip[st, chip] = y_part[st] + y_pair[st]
        for i in range(3):
            y_chip_copy(st, i).start()

    def y_done(st):
        for i in range(3):
            y_chip_copy(st, i).wait_send()
            y_chip_copy(st, i).wait_recv()
        total = y_chip[st, 0]
        for i in range(1, n_chip):
            total = total + y_chip[st, i]
        y_row[...] = y_row[...] + total.astype(BF16).astype(F32)

        @pl.when(st < n_stage - 1)
        def _():
            at = jnp.where(st + 1 == swap_stage, grp * half + half, rows)
            put_y(gains[jnp.minimum(st + 1, n_stage - 1)], pl.multiple_of(at, PAD))

        @pl.when(st == n_stage - 1)
        def _():
            tail_out[:, pl.ds(0, d_model)] = y_row[...]
            tail_copy.start()

    def c0_copy(layer):
        src = kv0 if layer == 0 else kv1.at[0]
        return remote(src, cb0.at[layer], c0_s.at[layer], c0_r.at[layer], to_up)

    def c1_copy(layer, i):
        def tokens(c):
            return pl.ds(pl.multiple_of(c * tok_chip, tok_chip), tok_chip)

        src, dst, to = (
            (cb0.at[layer, :, tokens(c_right)], cb1.at[layer, 0], to_right),
            (cb0.at[layer, :, tokens(c_left)], cb1.at[layer, 1], to_left),
            (cb0.at[layer, 0, tokens(c_far)], relay.at[layer, 0], to_right),
            (cb0.at[layer, 1, tokens(c_far)], relay.at[layer, 1], to_left),
            (relay.at[layer, 0], cb1.at[layer, 2, 0], to_right),
            (relay.at[layer, 1], cb1.at[layer, 2, 1], to_left),
        )[i]
        return remote(src, dst, c1_s.at[layer, i], c1_r.at[layer, i], to)

    def c2_source(layer, i, n, which):
        off = pl.multiple_of(which * tok_dev, tok_dev)
        if i < 3:
            return cb1.at[layer, i, n, pl.ds(off, tok_dev)], (c_left, c_right, c_far)[i]
        return cb0.at[layer, n, pl.ds(pl.multiple_of(chip * tok_chip + off, tok_dev), tok_dev)], chip

    def c2_copy(layer, i, n):
        src, src_chip = c2_source(layer, i, n, 1 - core)
        return remote(src, (k_tok, v_tok)[n].at[layer, 2 * src_chip + core], c2_s.at[layer, i, n], c2_r.at[layer, i, n], to_pair)

    def c2_local(layer, i, n):
        src, src_chip = c2_source(layer, i, n, core)
        return pltpu.make_async_copy(src, (k_tok, v_tok)[n].at[layer, 2 * src_chip + core], c2_l.at[layer, i, n])

    def cache_events(g):
        for layer in range(n_layers):
            at = CACHE_STEPS[layer]

            @pl.when(g == at[0])
            def _():
                c0_copy(layer).start()

            @pl.when(g == at[1])
            def _():
                c0_copy(layer).wait_send()
                c0_copy(layer).wait_recv()
                c1_copy(layer, 0).start()
                c1_copy(layer, 1).start()

            @pl.when(g == at[2])
            def _():
                c1_copy(layer, 2).start()
                c1_copy(layer, 3).start()

            @pl.when(g == at[3])
            def _():
                for i in (2, 3):
                    c1_copy(layer, i).wait_send()
                    c1_copy(layer, i).wait_recv()
                for i in (4, 5):
                    c1_copy(layer, i).start()

            @pl.when(g == at[4])
            def _():
                for i in (0, 1, 4, 5):
                    c1_copy(layer, i).wait_send()
                    c1_copy(layer, i).wait_recv()
                for i in range(4):
                    for n in range(2):
                        c2_copy(layer, i, n).start()
                        c2_local(layer, i, n).start()

            @pl.when(g == at[5])
            def _():
                for i in range(4):
                    for n in range(2):
                        c2_copy(layer, i, n).wait_send()
                        c2_copy(layer, i, n).wait_recv()
                        c2_local(layer, i, n).wait()

    n_wq = n_slots
    n_wx = len(WX_STEPS)
    o_piece = o_rows // n_ho // (n_wx - n_wq)

    def wx_ref(i, quarter, first=0, parts=1, given=False):
        size = (d_model // n_ho if i < n_wq else o_piece) // parts
        if i < n_wq:
            base = quarter * (d_model // n_ho)
            ref = w_qkv.at[swap_layer, i] if given else wq_x.at[i]
        else:
            base = quarter * (o_rows // n_ho) + (i - n_wq) * o_piece
            ref = w_o.at[swap_layer] if given else wo_x
        return ref.at[pl.ds(pl.multiple_of(base + first * size, size), size)]

    def wx_copy(i):
        return remote(wx_ref(i, ho, given=True), wx_ref(i, ho), wx_s.at[i], wx_r.at[i], to_swap)

    def wy_copy(i, j):
        ref = (
            wx_ref(i, ho),
            wx_ref(i, ho),
            wx_ref(i, lax.rem(ho + n_ho - 1, n_ho), 0, 2),
            wx_ref(i, lax.rem(ho + 1, n_ho), 1, 2),
        )[j]
        return remote(ref, ref, wy_s.at[i, j], wy_r.at[i, j], (to_up, to_down)[j % 2])

    def swap_events(g):
        for i in range(n_wx):
            @pl.when(g == WX_STEPS[i])
            def _():
                wx_copy(i).start()

    def share_events(g):
        for i in range(n_wx):
            share = WX_STEPS[i] + 2 + (i == n_wx - 2)

            @pl.when(g == share)
            def _():
                wx_copy(i).wait_send()
                wx_copy(i).wait_recv()
                for j in (0, 1):
                    wy_copy(i, j).start()

            @pl.when(g == share + 1)
            def _():
                for j in (0, 1):
                    wy_copy(i, j).wait_send()
                    wy_copy(i, j).wait_recv()
                for j in (2, 3):
                    wy_copy(i, j).start()

    def swap_arrived(pieces):
        for i in pieces:
            for j in (2, 3):
                wy_copy(i, j).wait_send()
                wy_copy(i, j).wait_recv()

    def store_part(g, t, acc):
        cols = pl.ds(pl.multiple_of(t * COLS_B, COLS_B), COLS_B)
        part[lax.rem(g, 3), :, :, :, cols] = acc[:rows].astype(BF16).reshape(2, 2, seg, COLS_B)
        y_part[lax.div(g, CHUNKS), :, cols] = acc[rows:rows + 1]

    def first_norm(c):
        prompt_copy(c).wait()
        gain = gains[0]
        for i in range(own // PAD):
            resid[c, pl.ds(i * PAD, PAD)] = hid[c, pl.ds(pl.multiple_of(block_row(chip, core) + i * PAD, PAD), PAD)]

        @pl.loop(0, rows // NORM_ROWS)
        def _(i):
            loc = pl.ds(pl.multiple_of(i * NORM_ROWS, NORM_ROWS), NORM_ROWS)
            hid[c, loc] = norm_rows(hid[c, loc].astype(F32), gain)

        @pl.when(c == CHUNKS - 1)
        def _():
            first_copy.wait_send()
            first_copy.wait_recv()
            put_y(gain, rows)

    def attention(c, keys, n_rows, row_of, before_diag, put):
        units = range(len(keys))

        def loc_of(j):
            return pl.ds(pl.multiple_of(j * rows, rows), rows)

        def score(u, loc):
            return lax.dot_general(qry[pl.ds(u * n_rows, n_rows)], keys[u][0, loc], CONTRACT_LAST, preferred_element_type=F32) * scale

        def fold(op, x, s):
            for b in range(rows // head):
                x = op(x, s[:, b * head:(b + 1) * head])
            return x

        def first(j, tops):
            loc = loc_of(j)
            new = []
            for u in units:
                s = score(u, loc)
                scores[pl.ds(u * n_rows, n_rows), loc] = s
                new.append(fold(jnp.maximum, tops[u], s))
            return tuple(new)

        lowest = jnp.full((n_rows, head), -jnp.inf, F32)
        tops = lax.fori_loop(0, c, first, tuple(lowest for _ in units))
        before_diag()
        diag = loc_of(c)
        causal = row_of(lax.broadcasted_iota(jnp.int32, (n_rows, rows), 0)) >= lax.broadcasted_iota(jnp.int32, (n_rows, rows), 1)
        row_top = []
        for u in units:
            s = jnp.where(causal, score(u, diag), -jnp.inf)
            scores[pl.ds(u * n_rows, n_rows), diag] = s
            row_top.append(jnp.max(fold(jnp.maximum, tops[u], s), axis=1, keepdims=True))

        def second(j, carry):
            loc = loc_of(j)
            new = []
            for u in units:
                denom, numer = carry[u]
                p = jnp.exp(scores[pl.ds(u * n_rows, n_rows), loc] - row_top[u])
                new.append((fold(jnp.add, denom, p), numer + jnp.dot(p.astype(BF16), keys[u][1, loc], preferred_element_type=F32)))
            return tuple(new)

        zero = jnp.zeros((n_rows, head), F32)
        sums = lax.fori_loop(0, c + 1, second, tuple((zero, zero) for _ in units))
        for u in units:
            denom, numer = sums[u]
            put(u, (numer / jnp.sum(denom, axis=1, keepdims=True)).astype(BF16))

    def attention_new(keys, att, at):
        q = qry_new[...].reshape(n_group * PAD, head)
        k_row = k_new[...].astype(F32)[:1]
        v_row = v_new[...].astype(F32)[:1]
        s_new = jnp.sum(q.astype(F32) * k_row, axis=1, keepdims=True) * scale
        s_old = lax.dot_general(q, keys[0], CONTRACT_LAST, preferred_element_type=F32) * scale
        top = jnp.maximum(jnp.max(s_old, axis=1, keepdims=True), s_new)
        p_old = jnp.exp(s_old - top)
        p_new = jnp.exp(s_new - top)
        denom = jnp.sum(p_old, axis=1, keepdims=True) + p_new
        numer = jnp.dot(p_old.astype(BF16), keys[1], preferred_element_type=F32) + p_new * v_row
        out = (numer / denom).astype(BF16)
        for h in range(n_group):
            att[pl.ds(at, PAD), pl.ds(h * head, head)] = out[h * PAD:(h + 1) * PAD]

    def put_new_kv(layer):
        tail_out[:, pl.ds(d_model + 2 * layer * head, head)] = k_new[...].astype(F32)[:1]
        tail_out[:, pl.ds(d_model + (2 * layer + 1) * head, head)] = v_new[...].astype(F32)[:1]

    def next_is_mlp(layer, c):
        @pl.when(c == CHUNKS - 1)
        def _():
            for t in range(2):
                start_gu(layer, t)

    def step_a(g, c):
        layer = 0
        first_norm(c)

        @pl.when(c == 0)
        def _():
            for t in range(t_qkv):
                for u in range(2):
                    qkv_copy(layer, t, u).wait()

        for t in range(t_qkv):
            out = jnp.dot(hid[c], wa[t], preferred_element_type=F32).astype(BF16)
            if t < t_qkv - 1:
                for u in range(2):
                    h = 2 * t + u
                    qry[pl.ds(h * rows, rows)] = out[:rows, u * head:(u + 1) * head]
                    qry_new[h] = out[rows:, u * head:(u + 1) * head]
            else:
                loc = pl.ds(pl.multiple_of(c * rows, rows), rows)
                kv0[0, loc] = out[:rows, :head]
                kv0[1, loc] = out[:rows, head:]
                k_new[...] = out[rows:, :head]
                v_new[...] = out[rows:, head:]

        next_is_mlp(layer, c)
        when_chunk(g - 1, e1)

        def put(u, o):
            att0[pl.ds(0, rows), pl.ds(u * head, head)] = o

        attention(c, [kv0] * n_group, rows, lambda r: r, lambda: None, put)

        @pl.when(c == CHUNKS - 1)
        def _():
            attention_new(kv0, att0, rows)
            put_new_kv(layer)

        @pl.when(c == 0)
        def _():
            for t in range(t_out):
                out_copy(layer, t).wait()

        for t in range(t_out):
            store_part(g, t, jnp.dot(att0[...], out_tile(t)[...], preferred_element_type=F32))

        @pl.when(c == CHUNKS - 1)
        def _():
            for t in range(SLOTS_B):
                down_copy(layer, 0, t).start()

    def kx_copy(c, o):
        loc = pl.ds(pl.multiple_of(c * rows + grp * half, half), half)
        return remote(kv1.at[o, :, loc], kv1.at[1 - o, :, loc], kx_s.at[o], kx_r.at[c, 1 - o], to_swap)

    def swap_qkv(c):
        lhs = pl.ds(pl.multiple_of(grp * half, half), half + PAD)
        loc = pl.ds(pl.multiple_of(c * rows + grp * half, half), half)
        for pair in range(t_qkv):
            slot = lax.rem(c * t_qkv + pair, 2) * 2
            for v in range(2):
                t = 2 * pair + v
                for u in range(2):
                    swap_qkv_copy(slot + v, t, u).wait()
                out = jnp.dot(hid[c, lhs], wa[slot + v], preferred_element_type=F32).astype(BF16)
                o, r = t // t_qkv, t % t_qkv
                if r < t_qkv - 1:
                    for u in range(2):
                        h = 2 * r + u
                        qry[pl.ds((o * n_group + h) * half, half)] = out[:half, u * head:(u + 1) * head]
                        if o == 0:
                            qry_new[h] = out[half:, u * head:(u + 1) * head]
                else:
                    kv1[o, 0, loc] = out[:half, :head]
                    kv1[o, 1, loc] = out[:half, head:]
                    if o == 0:
                        k_new[...] = out[half:, :head]
                        v_new[...] = out[half:, head:]

            if pair + 2 < t_qkv:
                start_swap_qkv(c, pair + 2)
            else:
                @pl.when(c + 1 < CHUNKS)
                def _():
                    start_swap_qkv(c + 1, pair + 2 - t_qkv)

        for o in range(2):
            kx_copy(c, o).start()

    def step_s(g, c):
        def before_diag():
            for o in range(2):
                kx_copy(c, o).wait_send()
                kx_copy(c, 1 - o).wait_recv()

        def put(u, out):
            for h in range(n_group):
                att1[pl.ds(0, half), pl.ds((u * n_group + h) * head, head)] = out[h * half:(h + 1) * half]

        attention(c, [kv1.at[0], kv1.at[1]], n_group * half, lambda r: lax.rem(r, half) + grp * half, before_diag, put)

        @pl.when(c == CHUNKS - 1)
        def _():
            attention_new(kv1.at[0], att1, half)
            put_new_kv(swap_layer)

        when_chunk(g - 1, e1)

    def swap_out(g, c):
        @pl.when(c == 0)
        def _():
            swap_arrived(range(n_wq, n_wx))
            for t in range(SLOTS_B):
                for v in range(2):
                    swap_out_copy(0, t, v).start()

        for t in range(t_out):
            slot = lax.rem(c * t_out + t, SLOTS_B)
            for v in range(2):
                swap_out_copy(c, t, v).wait()
            cols = pl.ds(t * COLS_B, COLS_B)
            acc = jnp.dot(att1[...], wb[slot, pl.ds(0, 2 * o_rows)], preferred_element_type=F32)
            part[lax.rem(g, 3), grp, :, :, cols] = acc[:half].astype(BF16).reshape(2, seg, COLS_B)
            y_part[swap_stage, :, cols] = acc[half:half + 1]
            ahead = t + SLOTS_B
            if ahead < t_out:
                for v in range(2):
                    swap_out_copy(c, ahead, v).start()
            else:
                @pl.when(c + 1 < CHUNKS)
                def _():
                    for v in range(2):
                        swap_out_copy(c + 1, ahead - t_out, v).start()

        @pl.when(c == CHUNKS - 1)
        def _():
            for t in range(SLOTS_B):
                down_copy(swap_layer, 0, t).start()

    def step_m(g, layer, c):
        more = layer < swap_layer

        @pl.loop(0, t_gu)
        def _(t):
            for u in range(2):
                gu_copy(layer, t, u).wait()
            slot = lax.rem(t, 2) * 2
            gate = jnp.dot(hid[c], wa[slot], preferred_element_type=F32)
            up = jnp.dot(hid[c], wa[slot + 1], preferred_element_type=F32)
            act[:, pl.ds(pl.multiple_of(t * COLS_A, COLS_A), COLS_A)] = (jax.nn.silu(gate) * up).astype(BF16)

            @pl.when(jnp.logical_or(t + 2 < t_gu, c + 1 < CHUNKS))
            def _():
                start_gu(layer, lax.rem(t + 2, t_gu))

        @pl.when(jnp.logical_and(c == CHUNKS - 1, more))
        def _():
            swap_arrived(range(n_wq))
            start_swap_qkv(0, 0)

        when_chunk(g - 1, e1)

        @pl.loop(0, t_out)
        def _(t):
            down_copy(layer, c, t).wait()
            store_part(g, t, jnp.dot(act[...], wb[lax.rem(c * t_out + t, SLOTS_B)], preferred_element_type=F32))
            ahead = t + SLOTS_B

            @pl.when(jnp.logical_or(ahead < t_out, c + 1 < CHUNKS))
            def _():
                down_copy(layer, c + lax.div(ahead, t_out), lax.rem(ahead, t_out)).start()

        @pl.when(jnp.logical_and(c == CHUNKS - 1, more))
        def _():
            start_swap_qkv(0, 1)

    for layer in range(n_layers):
        gains[2 * layer] = g_attn[layer:layer + 1]
        gains[2 * layer + 1] = g_mlp[layer:layer + 1]
    for c in range(CHUNKS):
        hid[c, pl.ds(rows, PAD)] = jnp.zeros((PAD, d_model), BF16)
    att0[pl.ds(rows, PAD)] = jnp.zeros((PAD, o_rows), BF16)
    att1[pl.ds(half, PAD)] = jnp.zeros((PAD, 2 * o_rows), BF16)
    pl.semaphore_wait(barrier, len(peers))
    first_copy.start()

    @pl.loop(0, n_steps + LAGS)
    def _(g):
        st = lax.div(g, CHUNKS)
        c = lax.rem(g, CHUNKS)
        layer = lax.div(st, 2)
        when_chunk(g - 6, e6)
        when_chunk(g - 5, e5)
        when_chunk(g - 4, e4)
        when_chunk(g - 3, e3)
        when_chunk(g - 2, e2)

        @pl.when(jnp.logical_and(c == 1, jnp.logical_and(st >= 1, st <= n_stage)))
        def _():
            y_sum(st - 1)

        @pl.when(jnp.logical_and(c == 2, jnp.logical_and(st >= 1, st <= n_stage)))
        def _():
            y_done(st - 1)

        share_events(g)

        @pl.when(g == 0)
        def _():
            swap_events(g)

        @pl.when(st == 0)
        def _():
            step_a(g, c)

        @pl.when(st == swap_stage)
        def _():
            step_s(g, c)

        @pl.when(jnp.logical_and(g < n_steps, lax.rem(st, 2) == 1))
        def _():
            step_m(g, layer, c)

        first_swap = swap_stage * CHUNKS - 1

        @pl.when(jnp.logical_and(g >= first_swap, g < first_swap + CHUNKS))
        def _():
            swap_qkv(g - first_swap)

        @pl.when(st == swap_stage)
        def _():
            swap_out(g, c)

        @pl.when(g == first_swap + CHUNKS - 1)
        def _():
            next_is_mlp(swap_layer, CHUNKS - 1)

        @pl.when(g > 0)
        def _():
            swap_events(g)

        cache_events(g)

        @pl.when(g == n_steps)
        def _():
            e1(g - 1)

        @pl.when(g < n_steps)
        def _():
            e0(g)

        @pl.when(jnp.logical_and(g < n_steps, c == CHUNKS - 1))
        def _():
            y_pair_copy(st).start()

    tail_copy.wait_send()
    tail_copy.wait_recv()
    tail[...] = tail_in[...]


def finish_kernel(hid, tail, k_tok, v_tok, x_last, k_cache, v_cache, y_last, kv_new, by_head, by_token, x_sem, in_sem, out_sem):
    n_layers = k_tok.shape[0]
    rows = x_last.shape[0] // CHUNKS
    d_model = y_last.shape[1]
    head = k_tok.shape[3]

    def x_copy(c):
        return pltpu.make_async_copy(hid.at[c, pl.ds(0, rows)], x_last.at[pl.ds(c * rows, rows)], x_sem.at[c])

    def in_copy(n):
        return pltpu.make_async_copy((k_tok, v_tok)[n], by_head.at[n], in_sem.at[n])

    def out_copy(n):
        return pltpu.make_async_copy(by_token.at[n], (k_cache, v_cache)[n], out_sem.at[n])

    for n in range(2):
        in_copy(n).start()
    for c in range(CHUNKS):
        x_copy(c).start()
    y_last[...] = tail[:, :d_model]
    kv_new[...] = jnp.concatenate([tail[:, d_model + i * head:d_model + (i + 1) * head] for i in range(2 * n_layers)], axis=0).astype(BF16)
    for n in range(2):
        in_copy(n).wait()
        for layer in range(n_layers):
            by_token[n, layer] = jnp.transpose(by_head[n, layer], (1, 0, 2))
        out_copy(n).start()
    for n in range(2):
        out_copy(n).wait()
    for c in range(CHUNKS):
        x_copy(c).wait()


def solution(mesh):
    n_ho, n_tp = mesh.shape['ho'], mesh.shape['tp']
    row_axes = ('pairs', 'ho')
    in_specs = (P('pairs'), P(row_axes), P(None, None, 'tp'), P(None, 'tp'), P(None, None, 'tp'), P(None, None, 'tp'), P(None, 'tp'), P(), P())
    out_specs = (P(row_axes), P(row_axes), P(row_axes, None, 'tp'), P(row_axes, None, 'tp'), P(row_axes, None, None, 'tp'))

    def device_program(prompts, y_first, w_qkv, w_o, w_gate, w_up, w_down, g_attn, g_mlp):
        n_layers, d_model, _, n_slots, head = w_qkv.shape
        n_tok = prompts.shape[1]
        ff = w_gate.shape[2]
        rows = n_tok // CHUNKS
        half = rows // 2
        seg = half // 2
        own = half // (n_tp // 2)
        n_stage = 2 * n_layers
        group = n_slots - 2
        o_rows = group * head
        tok_dev = n_tok // n_tp
        n_wx = len(WX_STEPS)
        wq = jnp.transpose(w_qkv[:, :, 0], (0, 2, 1, 3))
        tail_len = d_model + 2 * n_layers * head
        any_spec = pl.BlockSpec(memory_space=pl.ANY)
        vmem_spec = pl.BlockSpec(memory_space=pltpu.VMEM)
        hbm_spec = pl.BlockSpec(memory_space=pltpu.HBM)
        dma = pltpu.SemaphoreType.DMA
        both, both_ways, by_chunk, by_chunk_two = dma((2,)), dma((2, 2)), dma((CHUNKS,)), dma((CHUNKS, 2))
        by_stage, by_layer, cache = dma((n_stage,)), dma((n_layers,)), dma((n_layers, 4, 2))
        vmem = pltpu.VMEM
        hid, tail, k_tok, v_tok, *_ = pl.pallas_call(
            functools.partial(group_kernel, n_ho, n_tp),
            out_shape=(
                vmem((CHUNKS, rows + PAD, d_model), BF16),
                jax.ShapeDtypeStruct((1, tail_len), F32),
                jax.ShapeDtypeStruct((n_layers, n_tp, tok_dev, head), BF16),
                jax.ShapeDtypeStruct((n_layers, n_tp, tok_dev, head), BF16),
                jax.ShapeDtypeStruct((n_slots, d_model, head), BF16),
                jax.ShapeDtypeStruct((o_rows, d_model), BF16),
                jax.ShapeDtypeStruct((n_layers, 2, n_tok, head), BF16),
                jax.ShapeDtypeStruct((n_layers, 3, 2, 2 * tok_dev, head), BF16),
                jax.ShapeDtypeStruct((n_layers, 2, 2 * tok_dev, head), BF16),
            ),
            in_specs=[any_spec, vmem_spec, any_spec, any_spec, any_spec, any_spec, any_spec, vmem_spec, vmem_spec],
            out_specs=(vmem_spec, vmem_spec) + (any_spec,) * 7,
            scratch_shapes=[
                vmem((3, 2, 2, seg, d_model), BF16),
                vmem((2, 2, seg, d_model), BF16),
                vmem((2, 2, own // 2, d_model), BF16),
                vmem((2, 2, own, d_model), BF16),
                vmem((CHUNKS, own, d_model), BF16),
                vmem((2, n_tok, head), BF16),
                vmem((2, 2, n_tok, head), BF16),
                vmem((group * rows, n_tok), F32),
                vmem((group * rows, head), BF16),
                vmem((group, PAD, head), BF16),
                vmem((rows + PAD, o_rows), BF16),
                vmem((half + PAD, 2 * o_rows), BF16),
                vmem((rows + PAD, ff), BF16),
                vmem((4, d_model, COLS_A), BF16),
                vmem((SLOTS_B, ff, COLS_B), BF16),
                vmem((PAD, head), BF16),
                vmem((PAD, head), BF16),
                vmem((n_stage, 1, d_model), F32),
                vmem((1, d_model), F32),
                vmem((n_stage, 1, d_model), F32),
                vmem((n_stage, 1, d_model), F32),
                vmem((n_stage, n_tp // 2, 1, d_model), F32),
                vmem((1, tail_len), F32),
                vmem((1, tail_len), F32),
                dma((4, 2)), dma((2 * SLOTS_B,)), by_chunk,
                both, both, both, both_ways, both, both_ways,
                both, by_chunk_two, both, by_chunk_two, dma((4,)), dma((CHUNKS, 4)),
                by_stage, by_stage, dma((3,)), dma((n_stage, 3)), both, both,
                by_layer, by_layer, dma((n_layers, 6)), dma((n_layers, 6)),
                cache, cache, cache,
                both, by_chunk_two, dma((n_wx,)), dma((n_wx,)), dma((n_wx, 4)), dma((n_wx, 4)),
            ],
            compiler_params=pltpu.CompilerParams(collective_id=0, has_side_effects=True, vmem_limit_bytes=VMEM_LIMIT),
            name="group_step",
        )(prompts, y_first, wq, w_o, w_gate, w_up, w_down, g_attn, g_mlp)
        x_last, k_cache, v_cache, y_last, kv_new = pl.pallas_call(
            finish_kernel,
            out_shape=(
                jax.ShapeDtypeStruct((n_tok, d_model), BF16),
                jax.ShapeDtypeStruct((n_layers, tok_dev, n_tp, head), BF16),
                jax.ShapeDtypeStruct((n_layers, tok_dev, n_tp, head), BF16),
                jax.ShapeDtypeStruct((1, d_model), F32),
                jax.ShapeDtypeStruct((2 * n_layers, head), BF16),
            ),
            in_specs=[any_spec, vmem_spec, hbm_spec, hbm_spec],
            out_specs=(any_spec, any_spec, any_spec, vmem_spec, vmem_spec),
            scratch_shapes=[
                vmem((2, n_layers, n_tp, tok_dev, head), BF16),
                vmem((2, n_layers, tok_dev, n_tp, head), BF16),
                by_chunk, both, both,
            ],
            compiler_params=pltpu.CompilerParams(vmem_limit_bytes=16 << 20),
            name="finish",
        )(hid, tail, k_tok, v_tok)
        kv_new = kv_new.reshape(n_layers, 2, 1, head)
        return x_last[None], y_last, k_cache[None], v_cache[None], kv_new[None]

    return jax.shard_map(device_program, mesh=mesh, in_specs=in_specs, out_specs=out_specs, check_vma=False)
```

time: 612 us -> 594 us (0.971)
  local copies, waits for them, and re-layouts: 12.9 us -> 3.16 us
  Pallas kernels: 598 us -> 590 us
    slice x3 -> x0, local copies, waits for them, and re-layouts: 9.57 us -> none  [the longest x1 6.84 us: device_program(): x_last = hid[:, :rows].reshape(n_tok, d_model)]
    pallas_call x1 -> x2, Pallas kernels: 598 us -> 590 us  [the longest x1 583 us: device_program(): pl.pallas_call(functools.partial(group_kernel, n_ho, n_tp), out_shape=(vm...]
where the time goes in v3:
time: 594 us
  Pallas kernels  590 us (99%)
    pallas_call x1, Pallas kernels, device_program(): pl.pallas_call(functools.partial(group_kernel, n_ho, n_tp), out_shape=(vm...  583 us

profile of v3, /device:TPU:97, one launch (start us, length us, event | category | flops | bytes accessed | tf_op | source)
XLA Modules:
  0.0 593.8 jit_solution(1690904535068868483)
XLA Ops:
  0.6 582.7 %group_step.1 = (bf16[8,272,4096]{2,1,0:T(8,128)(2,1)S(1)}, f32[1,4608]{1,0:T(1,128)}, bf16[2,8,256,128]{3,2,1,0:T(8,128)(2,1)}, bf16[2,8,256,128]{3,2,1,0:T(8,1...) custom-call(bf16[4,2048,4096]{2,1,0:T(8,128)(2,1)} %prompts.1, ...), custom_call_target="tpu_custom_call" | custom-call | tf_op jit(solution)/shard_map/group_step/pallas_call | solution.py:933
  583.3 0.0 copy-start
  583.3 1.2 copy-done
  584.5 0.0 copy-start.1
  584.5 1.2 copy-done.1
  585.7 0.0 copy-start.2
  585.7 0.7 copy-done.2
  586.5 7.3 %finish.1 = (bf16[2048,4096]{1,0:T(8,128)(2,1)}, bf16[2,256,8,128]{3,2,1,0:T(8,128)(2,1)}, bf16[2,256,8,128]{3,2,1,0:T(8,128)(2,1)}, f32[1,4096]{1,0:T(1,128)}, bf16[4,128]{1,0:T(4,128)(2,1)}) custom-call(bf16[8,272,4096]{2,1,0:T(8,128)(2,1)S(1)} %get-tuple-element.14.hid, f32[1,4608]{1,0:T(1,128)S(1)} %copy-done.2, bf16[2,8,256,128]{3,2,1,0:T(8,128)(2,1)S(1)} %copy-done, ...), custom_call_target="tpu_custom_call" | custom-call | tf_op jit(solution)/shard_map/finish/pallas_call | solution.py:984
Async XLA Ops:
  583.3 1.2 copy-start
  584.5 1.2 copy-start.1
  585.7 0.7 copy-start.2

commit v4 on v3

--- a/solution.py
+++ b/solution.py
@@ -934,7 +934,7 @@
             functools.partial(group_kernel, n_ho, n_tp),
             out_shape=(
                 vmem((CHUNKS, rows + PAD, d_model), BF16),
-                jax.ShapeDtypeStruct((1, tail_len), F32),
+                vmem((1, tail_len), F32),
                 jax.ShapeDtypeStruct((n_layers, n_tp, tok_dev, head), BF16),
                 jax.ShapeDtypeStruct((n_layers, n_tp, tok_dev, head), BF16),
                 jax.ShapeDtypeStruct((n_slots, d_model, head), BF16),
@@ -999,7 +999,7 @@
             ],
             compiler_params=pltpu.CompilerParams(vmem_limit_bytes=16 << 20),
             name="finish",
-        )(hid, tail, k_tok, v_tok)
+        )(hid, tail, *(pltpu.with_memory_space_constraint(tokens, pltpu.HBM) for tokens in (k_tok, v_tok)))
         kv_new = kv_new.reshape(n_layers, 2, 1, head)
         return x_last[None], y_last, k_cache[None], v_cache[None], kv_new[None]
 

time: 594 us -> 590 us (level)
  no operation moved by 1% of the time
where the time goes in v4:
time: 590 us
  Pallas kernels  589 us (100%)
    pallas_call x1, Pallas kernels, device_program(): pl.pallas_call(functools.partial(group_kernel, n_ho, n_tp), out_shape=(vm...  582 us

profile of v4, /device:TPU:97, one launch (start us, length us, event | category | flops | bytes accessed | tf_op | source)
XLA Modules:
  0.0 590.1 jit_solution(222174485206206376)
XLA Ops:
  0.6 582.2 %group_step.1 = (bf16[8,272,4096]{2,1,0:T(8,128)(2,1)S(1)}, f32[1,4608]{1,0:T(1,128)S(1)}, bf16[2,8,256,128]{3,2,1,0:T(8,128)(2,1)}, bf16[2,8,256,128]{3,2,1,0:T...) custom-call(bf16[4,2048,4096]{2,1,0:T(8,128)(2,1)} %prompts.1, ...), custom_call_target="tpu_custom_call" | custom-call | tf_op jit(solution)/shard_map/group_step/pallas_call | solution.py:933
  582.8 7.3 %finish.1 = (bf16[2048,4096]{1,0:T(8,128)(2,1)}, bf16[2,256,8,128]{3,2,1,0:T(8,128)(2,1)}, bf16[2,256,8,128]{3,2,1,0:T(8,128)(2,1)}, f32[1,4096]{1,0:T(1,128)}, bf16[4,128]{1,0:T(4,128)(2,1)}) custom-call(bf16[8,272,4096]{2,1,0:T(8,128)(2,1)S(1)} %get-tuple-element.14.hid, f32[1,4608]{1,0:T(1,128)S(1)} %get-tuple-element.15.tail, ...), custom_call_target="tpu_custom_call" | custom-call | tf_op jit(solution)/shard_map/finish/pallas_call | solution.py:984
